TPU v7x, 256 devices: a whole 4x4x8 slice. The times are simulated.
256 devices in a mesh: gx: 8 (over y, core), gy: 32 (over x, z).
Axes of the slice: x: 4, y: 4, z: 8, core: 2. Of those that a mesh axis runs over, the one named last changes fastest.
Arguments:
- source: float32 [64, 32, 4096], P(None, 'gx', 'gy'), may hold values from -6 to 6
- initial: float32 [64, 32, 4096], P(None, 'gx', 'gy'), may hold values from -6 to 6
- reaction: float32 [64, 32, 4096], P(None, 'gx', 'gy'), may hold values from 1 to 3
- stiffness: float32 [32, 4096], P('gx', 'gy'), may hold values from 0.5 to 2
- line_op: float32 [8, 8], replicated, may hold values from -1.6 to 5.6
- face_deriv: float32 [8], replicated, may hold values from -2 to 2
- wall_flags: int32 [4, 32, 4096], P(None, 'gx', 'gy'), may hold values 0 or 1
Outputs:
- hessenberg: float32 [6, 5], replicated
- krylov_basis: float32 [6, 64, 32, 4096], P(None, None, 'gx', 'gy')
All inputs are finite; a program needn't handle non-finite values. No bound on the sum of `wall_flags` on one device may be relied on, other than what follows from the above.
Results may differ from a plain program's by a relative error of at most 0.0003.
Values sent between devices are 32-bit elements; how exact they have to be, the bound alone decides.
No kernel may reach another device: no remote copies, remote signals or barrier semaphores. Data moves between devices by JAX's collectives and lax.ppermute only.
A program may use at most 64 MiB of HBM per device.

v0:
```python
import functools

import jax
import jax.numpy as jnp
from jax import lax
from jax.experimental import pallas as pl
from jax.experimental.pallas import tpu as pltpu
from jax.sharding import Mesh
from jax.sharding import PartitionSpec as P

P_SIZE = 8
ITERS = 5
GX = ("gx_0", "gx_1")
GY = ("gy_0", "gy_1")


TAU = 2.0
FLOOR = 0.1


def extended(array, sides, width):
    for axis, dim in sides:
        devices, length = (lax.axis_size(axis), array.shape[dim])
        up = [(i, (i + 1) % devices) for i in range(devices)]
        down = [(j, i) for i, j in up]
        last = lax.slice_in_dim(array, length - width, length, axis=dim)
        leading = lax.slice_in_dim(array, 0, width, axis=dim)
        before = lax.ppermute(last, axis, up)
        after = lax.ppermute(leading, axis, down)
        array = jnp.concatenate([before, array, after], axis=dim)
    return array


def sent_to_all(array, axis):
    copies = jnp.broadcast_to(array, (lax.axis_size(axis), *array.shape))
    return lax.all_to_all(copies, axis, split_axis=0, concat_axis=0, tiled=True)


def over_copies(array, axis):
    everything = sent_to_all(array, axis)
    return jnp.sum(everything, axis=0)


def by_axis(array, axes):
    far, near = axes
    nearer = over_copies(array, near)
    return over_copies(nearer, far)


def together(arrays, axis):
    vector, at, gathered = (jnp.concatenate([a.reshape(-1) for a in arrays]), 0, [])
    subtotal = by_axis(vector, axis)
    for a in arrays:
        gathered.append(subtotal[at : at + a.size].reshape(a.shape))
        at += a.size
    return tuple(gathered)


def local_total(values):
    return jnp.sum(jnp.sum(values, axis=0))


def x_traces(nodes, face_deriv):
    highest = lax.Precision.HIGHEST
    lower = jnp.einsum("c,cbxy->bxy", face_deriv, nodes, precision=highest)
    upper = jnp.einsum("c,cbxy->bxy", face_deriv[::-1], nodes, precision=highest)
    return jnp.stack([nodes[0], lower, nodes[-1], upper])


def y_traces(nodes, face_deriv):
    highest = lax.Precision.HIGHEST
    lower = jnp.einsum("c,acxy->axy", face_deriv, nodes, precision=highest)
    upper = jnp.einsum("c,acxy->axy", face_deriv[::-1], nodes, precision=highest)
    return jnp.stack([nodes[:, 0], lower, nodes[:, -1], upper])


def apply_op(field, reaction, stiffness, line_op, face_deriv, opened):
    highest = lax.Precision.HIGHEST
    nodes = field.reshape(P_SIZE, P_SIZE, field.shape[1], field.shape[2])
    interior = stiffness * (
        jnp.einsum("ac,cbxy->abxy", line_op, nodes, precision=highest)
        + jnp.einsum("bc,acxy->abxy", line_op, nodes, precision=highest)
    )
    xside = extended(x_traces(nodes, face_deriv), ((GX, 2),), 1)
    yside = extended(y_traces(nodes, face_deriv), ((GY, 3),), 1)
    x_own = xside[:, :, 1:-1]
    y_own = yside[:, :, :, 1:-1]
    east_nb = xside[0:2, :, 2:]
    west_nb = xside[2:4, :, :-2]
    north_nb = yside[0:2, :, :, 2:]
    south_nb = yside[2:4, :, :, :-2]
    add_east = TAU * (x_own[2] - opened[1] * east_nb[0]) + 0.5 * (x_own[3] - opened[1] * east_nb[1])
    add_west = TAU * (x_own[0] - opened[0] * west_nb[0]) + 0.5 * (x_own[1] - opened[0] * west_nb[1])
    add_north = TAU * (y_own[2] - opened[3] * north_nb[0]) + 0.5 * (
        y_own[3] - opened[3] * north_nb[1]
    )
    add_south = TAU * (y_own[0] - opened[2] * south_nb[0]) + 0.5 * (
        y_own[1] - opened[2] * south_nb[1]
    )
    result = reaction.reshape(nodes.shape) * nodes + interior
    result = result.at[0].add(add_west).at[P_SIZE - 1].add(add_east)
    result = result.at[:, 0].add(add_south).at[:, P_SIZE - 1].add(add_north)
    return result.reshape(field.shape)


def norm_scale(vector, total):
    squares = by_axis(local_total(vector * vector), (("gx_0", "gx_1"), ("gy_0", "gy_1")))
    return jnp.sqrt(squares / total + FLOOR)


def stepwise(source, initial, reaction, stiffness, line_op, face_deriv, opened):
    highest = lax.Precision.HIGHEST
    total = float(
        P_SIZE * P_SIZE * source.shape[1] * lax.axis_size(GX) * source.shape[2] * lax.axis_size(GY)
    )

    def operate(field):
        return apply_op(field, reaction, stiffness, line_op, face_deriv, opened)

    def products(basis, image):
        per_cell = jnp.einsum("kqxy,qxy->kxy", basis, image, precision=highest)
        return jnp.sum(per_cell, axis=(1, 2))

    first = source - operate(initial)
    basis = jnp.zeros((ITERS + 1,) + source.shape, jnp.float32)
    hessen = jnp.zeros((ITERS + 1, ITERS), jnp.float32)
    rows = lax.broadcasted_iota(jnp.int32, (ITERS + 1, ITERS), 0)
    cols = lax.broadcasted_iota(jnp.int32, (ITERS + 1, ITERS), 1)
    slots = lax.broadcasted_iota(jnp.int32, (ITERS + 1,), 0)

    def advance(step, carry):
        basis, hessen, pending = carry
        image = operate(pending)
        local = products(basis, image)
        projected, crossed, squares = together(
            (local, local_total(pending * image), local_total(pending * pending)),
            (("gx_0", "gx_1"), ("gy_0", "gy_1")),
        )
        beta = jnp.sqrt(squares / total + FLOOR)
        basis = lax.dynamic_update_index_in_dim(basis, pending / beta, step, 0)
        coeffs = projected / (total * beta) + jnp.where(
            slots == step, crossed / (total * beta * beta), 0.0
        )
        pending = image / beta - jnp.einsum("k,kqxy->qxy", coeffs, basis, precision=highest)
        hessen = hessen + jnp.where(cols == step, coeffs[:, None], 0.0)
        hessen = hessen + jnp.where((rows == step) & (cols == step - 1), beta, 0.0)
        return (basis, hessen, pending)

    basis, hessen, pending = lax.fori_loop(0, ITERS, advance, (basis, hessen, first))
    beta = norm_scale(pending, total)
    basis = basis.at[ITERS].set(pending / beta)
    hessen = hessen + jnp.where((rows == ITERS) & (cols == ITERS - 1), beta, 0.0)
    return (hessen, basis)


NODES = P_SIZE * P_SIZE
ROWS = 16
DEPTH = 6
LANES = 128
SCALE = 0.125
AMP_LIMIT = 100.0
GRAM = [(k, l) for k in range(ITERS + 1) for l in range(k + 1)]


def lane_ids(rows):
    return lax.broadcasted_iota(jnp.int32, (rows, LANES), 1)


def turned(value, shift):
    shift = shift % LANES
    return value if shift == 0 else pltpu.roll(value, shift, 1)


def strided(ref, start, count):
    return ref[pl.ds(start, count, stride=4), :]


BLOCK = 136
REACT, THICK, OPEN = 64, 128, 129
FIRST_WEST, LAST_EAST, ENDS = 544, 552, 560


def split(value):
    high = value.astype(jnp.bfloat16)
    rest = value - high.astype(jnp.float32)
    middle = rest.astype(jnp.bfloat16)
    low = (rest - middle.astype(jnp.float32)).astype(jnp.bfloat16)
    return high, middle, low


def weights_in(line, deriv):
    sub = lax.broadcasted_iota(jnp.int32, (8, NODES), 0)
    lane = lax.broadcasted_iota(jnp.int32, (8, NODES), 1)
    along, across = lane // 8, lane % 8
    outer = jnp.zeros((8, NODES), jnp.float32)
    inner = jnp.zeros((8, NODES), jnp.float32)
    for c in range(P_SIZE):
        column = jnp.broadcast_to(line[:, c : c + 1], (8, NODES))
        outer = jnp.where(along == c, column, outer)
        inner = jnp.where(across == c, column, inner)
    parts = []
    for a in range(P_SIZE):
        row = jnp.broadcast_to(outer[a : a + 1, :], (8, NODES))
        parts.append(jnp.where(across == sub, row, 0.0) + jnp.where(along == a, inner, 0.0))
    for first, second in ((along, across), (across, along)):
        for flip in (False, True):
            part = jnp.zeros((8, NODES), jnp.float32)
            for c in range(P_SIZE):
                value = SCALE * (0.5 * deriv[0:1, c : c + 1] + (TAU if c == 0 else 0.0))
                part = jnp.where(first == (P_SIZE - 1 - c if flip else c), value, part)
            parts.append(jnp.where(second == sub, part, 0.0))
    high, middle, low = split(jnp.concatenate(parts, axis=0))
    return jnp.concatenate([high, high, high, middle, middle, low], axis=1)


def product(weight, value):
    high, middle, low = split(value)
    stacked = jnp.concatenate([high, middle, low, high, middle, high], axis=0)
    return jnp.dot(weight[...], stacked, preferred_element_type=jnp.float32)


def centre(line, deriv):
    diagonal = lax.broadcasted_iota(jnp.int32, (8, 8), 0) == lax.broadcasted_iota(jnp.int32, (8, 8), 1)
    trace = jnp.sum(jnp.where(diagonal, line, 0.0), axis=1, keepdims=True)
    trace = jnp.sum(trace, axis=0, keepdims=True)
    return 2.0 + 0.3125 * trace + 0.5 * (TAU + 0.5 * deriv[0:1, 0:1])


def edges(a, west, east, south, north, sub):
    value = jnp.where(sub == 0, south[a : a + 1, :], 0.0)
    value = jnp.where(sub == P_SIZE - 1, north[a : a + 1, :], value)
    if a == 0 and west is not None:
        value = value + west
    if a == P_SIZE - 1 and east is not None:
        value = value + east
    return value


def pack_kernel(
    line_in, deriv_in, source, initial, reaction, stiffness, walls,
    raw, near, to_up, to_down, weight, shift_out, line, deriv, flags, sems,
):
    moves = [(line_in, line), (deriv_in, deriv)]
    for at, ref in ((0, initial), (256, source), (512, reaction)):
        for half in (0, 128):
            moves.append((ref.at[pl.ds(half, 128), :], raw.at[pl.ds(at + half, 128), :]))
    moves.append((stiffness, raw.at[pl.ds(768, 4), :]))
    moves.append((walls, flags))
    copies = [pltpu.make_async_copy(a, b, sems.at[n]) for n, (a, b) in enumerate(moves)]
    for copy in copies:
        copy.start()
    for copy in copies[:2]:
        copy.wait()
    line, deriv = line[...], deriv[...]
    weight[...] = weights_in(line, deriv)
    shift_out[...] = jnp.broadcast_to(centre(line, deriv), (8, LANES))
    for copy in copies[2:4]:
        copy.wait()
    sub = lax.broadcasted_iota(jnp.int32, (8, LANES), 0)
    lanes8 = lane_ids(8)
    fields, images = [], []
    for x in range(0, 4, 2):
        pair = jnp.concatenate([strided(raw, x, NODES), strided(raw, x + 1, NODES)], axis=1)
        image = product(weight, pair)
        for k in range(2):
            fields.append(pair[:, k * LANES : (k + 1) * LANES])
            images.append(image[:, k * LANES : (k + 1) * LANES])
    for copy in copies[4:]:
        copy.wait()
    opened = 1.0 - flags[...].astype(jnp.float32)
    raw[772:788, :] = opened
    raw[788:796, 0:P_SIZE] = line
    raw[796:797, 0:P_SIZE] = deriv
    thick = raw[768:772, :]
    traces = [[image[64 + 8 * f : 72 + 8 * f] for f in range(4)] for image in images]
    ends = jnp.zeros((8, LANES), jnp.float32)
    for x in range(4):
        at = BLOCK * x
        allowed = [jnp.broadcast_to(opened[4 * f + x : 4 * f + x + 1, :], (8, LANES)) for f in range(4)]
        faces = list(traces[x])
        if x > 0:
            faces[0] = faces[0] - allowed[0] * traces[x - 1][1]
        if x < 3:
            faces[1] = faces[1] - allowed[1] * traces[x + 1][0]
        faces[2] = faces[2] - allowed[2] * jnp.where(lanes8 == 0, 0.0, turned(traces[x][3], 1))
        faces[3] = faces[3] - allowed[3] * jnp.where(lanes8 == LANES - 1, 0.0, turned(traces[x][2], -1))
        faces = [8.0 * face for face in faces]
        ends = jnp.where(lanes8 == 8 * x + 7, turned(traces[x][2], 8 * x + 7), ends)
        ends = jnp.where(lanes8 == 8 * x, turned(traces[x][3], 8 * x + 1), ends)
        width = jnp.broadcast_to(thick[x : x + 1, :], (8, LANES))
        for a in range(P_SIZE):
            rows = slice(8 * a, 8 * a + 8)
            value = strided(raw, 512 + 32 * a + x, 8) * fields[x][rows] + width * images[x][rows]
            value = value + edges(a, *faces, sub)
            near[at + 8 * a : at + 8 * a + 8, :] = strided(raw, 256 + 32 * a + x, 8) - value
        near[at + REACT : at + THICK, :] = strided(raw, 512 + x, NODES)
        rows = [thick[x : x + 1, :]] + [opened[4 * f + x : 4 * f + x + 1, :] for f in range(4)]
        near[at + THICK : at + BLOCK, :] = jnp.concatenate(rows + [jnp.zeros((3, LANES), jnp.float32)], axis=0)
    near[FIRST_WEST:LAST_EAST, :] = traces[0][0]
    near[LAST_EAST:ENDS, :] = traces[3][1]
    near[ENDS : ENDS + 8, :] = ends
    lanes = lane_ids(NODES)
    for out, first in ((to_up, 120), (to_down, 0)):
        totals = [jnp.zeros((n, LANES), jnp.float32) for n in (NODES, 32, 8)]
        for x in range(4):
            block = BLOCK * x
            parts = (
                (0, near[block : block + 64, :]),
                (0, near[block + REACT : block + THICK, :]),
                (1, jnp.concatenate(traces[x], axis=0)),
                (2, near[block + THICK : block + BLOCK, :]),
            )
            for field, (part, value) in enumerate(parts):
                at = 32 * field + 8 * x
                ids = lanes[0 : value.shape[0]]
                totals[part] = jnp.where((ids >= at) & (ids < at + 8), turned(value, at - first), totals[part])
        out[0:8, :] = totals[0][0:8] + totals[1][0:8] + totals[2]
        out[8:32, :] = totals[0][8:32] + totals[1][8:32]
        out[32:64, :] = totals[0][32:64]


def far_kernel(near, left, right, strip, high2, low2):
    lanes = lane_ids(NODES)
    strip[0:64, :] = jnp.where(lanes < 64, left[...], turned(right[...], 64))
    lanes = lanes[0:32]
    edge = jnp.where(lanes < 32, turned(left[0:32, :], -64), turned(right[0:32, :], -32))
    edge = jnp.where((lanes >= 64) & (lanes < 96), turned(left[0:32, :], -32), edge)
    edge = jnp.where(lanes >= 96, right[0:32, :], edge)
    strip[64:96, :] = edge
    for out, close, face in ((high2, 3, LAST_EAST), (low2, 0, FIRST_WEST)):
        block = BLOCK * close
        out[0:64, :] = near[block : block + 64, :]
        out[64:72, :] = near[block + THICK : block + BLOCK, :]
        out[72:80, :] = near[face : face + 8, :]
        out[80:88, :] = near[ENDS : ENDS + 8, :]
        out[88:120, :] = edge


def powers_kernel(
    shift_in, weight, near, below1, above1, below2, above2, own_strip, strip_b1, strip_a1,
    basis_out, gram_out, field_a, field_b, image, react, stiff, opened,
):
    shift = shift_in[0:1, :]

    def put(row, value_reaction, value_stiffness, value_open):
        cols = slice(row * LANES, (row + 1) * LANES)
        if value_reaction is not None:
            react[:, cols] = (value_reaction - shift) * SCALE
            stiff[:, cols] = jnp.broadcast_to(value_stiffness * SCALE, (8, LANES))
        for f in range(4):
            opened[8 * f : 8 * f + 8, cols] = jnp.broadcast_to(value_open[f], (8, LANES))

    local = {}
    for x in range(4):
        for ref, row in ((below1, 2 + x), (near, 6 + x), (above1, 10 + x)):
            at = BLOCK * x
            put(
                row, ref[at + REACT : at + THICK, :], ref[at + THICK : at + OPEN, :],
                [ref[at + OPEN + f : at + OPEN + f + 1, :] for f in range(4)],
            )
            local[row] = functools.partial(lambda ref, at, a: ref[at + 8 * a : at + 8 * a + 8, :], ref, at)
    for row, ref in ((1, below2), (ROWS - 2, above2)):
        put(row, None, None, [ref[65 + f : 66 + f, :] for f in range(4)])
        local[row] = functools.partial(lambda ref, a: ref[8 * a : 8 * a + 8, :], ref)

    lanes64 = lane_ids(NODES)
    lanes = lane_ids(8)
    pieces = ((strip_b1, 16, 48, 16), (own_strip, 48, 80, 48), (strip_a1, 80, 112, 80))
    strip_faces = []
    for side in range(2):
        made = []
        for top, count, zero in ((0, 64, 64 * side), (0, 64, 64 * side + 32), (64, 32, 32 * side), (64, 8, 64 + 32 * side)):
            ids = lanes64[0:count]
            value = jnp.zeros((count, LANES), jnp.float32)
            for ref, start, stop, target in pieces:
                part = turned(ref[top : top + count, :], target - zero)
                value = jnp.where((ids >= start) & (ids < stop), part, value)
            if count == 32:
                value = jnp.where(ids < 16, turned(below2[88:120, :], -16 - 32 * side), value)
                value = jnp.where(ids >= 112, turned(above2[88:120, :], 112 - 32 * side), value)
            made.append(value)
        put(ROWS + side, made[1], made[3][0:1], [made[3][1 + f : 2 + f] for f in range(4)])
        local[ROWS + side] = functools.partial(lambda value, a: value[8 * a : 8 * a + 8], made[0])
        strip_faces.append([made[2][8 * f : 8 * f + 8] for f in range(4)])
    ends = jnp.zeros((8, LANES), jnp.float32)
    for ref, top, start, stop, by in (
        (below2, 80, 0, 16, -16), (below1, ENDS, 16, 48, 16), (near, ENDS, 48, 80, 48),
        (above1, ENDS, 80, 112, 80), (above2, 80, 112, 128, 112),
    ):
        ends = jnp.where((lanes >= start) & (lanes < stop), turned(ref[top : top + 8, :], by), ends)

    def columns(row):
        return slice(row * LANES, (row + 1) * LANES)

    low, high = ROWS, ROWS + 1
    sub = lax.broadcasted_iota(jnp.int32, (8, LANES), 0)
    TW, TE, TS, TN = (slice(64 + 8 * f, 72 + 8 * f) for f in range(4))

    def begin(new):
        def finish(row, faces):
            cols = columns(row)
            faces = [
                None if value is None else 8.0 * opened[8 * f : 8 * f + 8, cols] * value
                for f, value in enumerate(faces)
            ]
            for a in range(P_SIZE):
                new[8 * a : 8 * a + 8, cols] = local[row](a) + edges(a, *faces, sub)

        west = {
            2: below2[72:80, :], 6: below1[LAST_EAST:ENDS, :], 10: near[LAST_EAST:ENDS, :],
            14: above1[LAST_EAST:ENDS, :],
        }
        east = {
            1: below1[FIRST_WEST:LAST_EAST, :], 5: near[FIRST_WEST:LAST_EAST, :],
            9: above1[FIRST_WEST:LAST_EAST, :], 13: above2[72:80, :],
        }
        for row in range(1, ROWS - 1):
            south = jnp.where(lanes == 0, turned(strip_faces[0][3], -(8 * row + 7)), 0.0)
            north = jnp.where(lanes == LANES - 1, turned(strip_faces[1][2], 127 - 8 * row), 0.0)
            finish(row, (west.get(row), east.get(row), south, north))
        none = jnp.zeros((8, LANES), jnp.float32)
        spot = lanes // 8 % 4
        for side in range(2):
            from_west = jnp.where(spot == 2, turned(strip_faces[side][1], 8), 0.0)
            from_east = jnp.where(spot == 1, turned(strip_faces[side][0], -8), 0.0)
            outer = jnp.where(lanes % 8 == (0 if side else 7), ends, 0.0)
            finish(ROWS + side, (from_west, from_east, outer if side else none, none if side else outer))

    def apply(old, new, step):
        start, stop = step, ROWS - step
        for first_row, last_row in ((start, stop), (ROWS, ROWS + 2)):
            for row in range(first_row, last_row, 2):
                cols = slice(row * LANES, (row + 2) * LANES)
                image[:, cols] = product(weight, old[:, cols])

        def finish(row, *sides):
            cols = columns(row)
            faces = [
                image[own, cols] - opened[8 * f : 8 * f + 8, cols] * value
                for f, (own, value) in enumerate(zip((TW, TE, TS, TN), sides))
            ]
            for a in range(P_SIZE):
                rows = slice(8 * a, 8 * a + 8)
                value = react[rows, cols] * old[rows, cols] + stiff[:, cols] * image[rows, cols]
                new[rows, cols] = value + edges(a, *faces, sub)

        north_low = image[TN, columns(low)]
        south_high = image[TS, columns(high)]
        for row in range(start + 1, stop - 1):
            cols = columns(row)
            from_south = jnp.where(
                lanes == 0, turned(north_low, -(8 * row + 7)), turned(image[TN, cols], 1)
            )
            from_north = jnp.where(
                lanes == LANES - 1, turned(south_high, 127 - 8 * row), turned(image[TS, cols], -1)
            )
            finish(row, image[TE, columns(row - 1)], image[TW, columns(row + 1)], from_south, from_north)
        if step == DEPTH - 1:
            return
        to_low = turned(image[TS, columns(low)], -1)
        to_high = turned(image[TN, columns(high)], 1)
        for row in range(start, stop):
            cols = columns(row)
            to_low = jnp.where(lanes == 8 * row + 7, turned(image[TS, cols], 8 * row + 7), to_low)
            to_high = jnp.where(lanes == 8 * row, turned(image[TN, cols], 8 * row + 1), to_high)
        cols = columns(low)
        finish(low, turned(image[TE, cols], 8), turned(image[TW, cols], -8), turned(image[TN, cols], 1), to_low)
        cols = columns(high)
        finish(high, turned(image[TE, cols], 8), turned(image[TW, cols], -8), to_high, turned(image[TS, cols], -1))

    old, new = field_a, field_b
    for step in range(DEPTH):
        if step:
            apply(old, new, step)
        else:
            begin(new)
        basis_out[step, :, :] = new[:, 6 * LANES : 10 * LANES]
        old, new = new, old

    sums = [jnp.zeros((8, LANES), jnp.float32) for _ in GRAM]
    for x in range(4):
        for a in range(P_SIZE):
            values = [basis_out[k, 8 * a : 8 * a + 8, x * LANES : (x + 1) * LANES] for k in range(ITERS + 1)]
            sums = [total + values[k] * values[l] for total, (k, l) in zip(sums, GRAM)]
    rows = [jnp.sum(total, axis=0, keepdims=True) for total in sums]
    rows = jnp.concatenate(rows + [jnp.zeros((24 - len(GRAM), LANES), jnp.float32)], axis=0)
    totals = jnp.sum(rows, axis=1, keepdims=True)
    place = lax.broadcasted_iota(jnp.int32, (24, LANES), 0) == lax.broadcasted_iota(jnp.int32, (24, LANES), 1)
    totals = jnp.sum(jnp.where(place, totals, 0.0), axis=0, keepdims=True)
    gram_out[...] = jnp.broadcast_to(totals, gram_out.shape)


def combine_kernel(nodes, shift_in, powers, gathered, basis_out, hess_out, amp_out):
    shift = shift_in[...]
    row = jnp.sum(gathered[...], axis=0, keepdims=True) * (1.0 / nodes)
    spread = jnp.broadcast_to(row, (8, LANES))
    gram = {}
    for at, (k, l) in enumerate(GRAM):
        gram[k, l] = gram[l, k] = jnp.broadcast_to(spread[:, at : at + 1], (8, LANES))
    sizes = [jnp.sqrt(gram[k, k]) for k in range(ITERS + 1)]
    sub = lax.broadcasted_iota(jnp.int32, (8, LANES), 0)
    lanes = lane_ids(8)
    hess = jnp.zeros((8, LANES), jnp.float32)
    beta = jnp.sqrt(gram[0, 0] + FLOOR)
    coeffs = [[1.0 / beta]]
    amp = sizes[0] * coeffs[0][0]

    def put(hess, i, j, value):
        return jnp.where((sub == i) & (lanes == j), value, hess)

    for j in range(ITERS):
        last = coeffs[j]
        image = [shift * c for c in last] + [None]
        for k in range(j + 1):
            moved = last[k] * 8.0
            image[k + 1] = moved if image[k + 1] is None else image[k + 1] + moved
        weighted = [
            sum(gram[k, l] * image[l] for l in range(1, j + 2)) + gram[k, 0] * image[0] for k in range(j + 2)
        ]
        pending = list(image)
        for i in range(j + 1):
            h = sum(c * weighted[k] for k, c in enumerate(coeffs[i]))
            hess = put(hess, i, j, h)
            for k, c in enumerate(coeffs[i]):
                pending[k] = pending[k] - h * c
        square = sum(
            pending[k] * sum(gram[k, l] * pending[l] for l in range(j + 2)) for k in range(j + 2)
        )
        beta = jnp.sqrt(jnp.maximum(square, 0.0) + FLOOR)
        hess = put(hess, j + 1, j, beta)
        scale = 1.0 / beta
        coeffs.append([p * scale for p in pending])
        amp = jnp.maximum(amp, sum(jnp.abs(c) * s for c, s in zip(coeffs[-1], sizes)))
    hess_out[...] = hess[0 : ITERS + 1, 0:ITERS]
    amp_out[...] = amp[0:1, :]
    for x in range(4):
        for a in range(P_SIZE):
            values = [powers[k, 8 * a : 8 * a + 8, x * LANES : (x + 1) * LANES] for k in range(ITERS + 1)]
            for j in range(ITERS + 1):
                total = coeffs[j][0] * values[0]
                for k in range(1, j + 1):
                    total = total + coeffs[j][k] * values[k]
                basis_out[j, pl.ds(32 * a + x, 8, stride=4), :] = total


def fast(source, initial, reaction, stiffness, line_op, face_deriv, walls):
    vmem = pl.BlockSpec(memory_space=pltpu.VMEM)
    hbm = pl.BlockSpec(memory_space=pltpu.HBM)
    grant = pltpu.CompilerParams(vmem_limit_bytes=16 * 2**20)
    f32 = jnp.float32
    nx, ny = lax.axis_size(GX), lax.axis_size(GY)
    wide = (ROWS + 2) * LANES

    def moved(value, axis, size, by):
        return lax.ppermute(value, axis, [(i, (i + by) % size) for i in range(size)])

    held = (line_op, face_deriv.reshape(1, P_SIZE), source, initial, reaction, stiffness, walls)
    raw, near, to_up, to_down, weight, shift = pl.pallas_call(
        pack_kernel,
        out_shape=[jax.ShapeDtypeStruct((n, LANES), f32) for n in (800, ENDS + 8, NODES, NODES)]
        + [jax.ShapeDtypeStruct((NODES + 32, 6 * NODES), jnp.bfloat16), jax.ShapeDtypeStruct((8, LANES), f32)],
        in_specs=[hbm] * 7,
        out_specs=[vmem] * 6,
        scratch_shapes=[
            pltpu.VMEM((P_SIZE, P_SIZE), f32),
            pltpu.VMEM((1, P_SIZE), f32),
            pltpu.VMEM((16, LANES), jnp.int32),
            pltpu.SemaphoreType.DMA((10,)),
        ],
        compiler_params=grant,
    )(*[pltpu.with_memory_space_constraint(v, pltpu.HBM) for v in held])
    left = moved(to_up, GY, ny, 1)
    right = moved(to_down, GY, ny, -1)
    below1 = moved(near, GX, nx, 1)
    above1 = moved(near, GX, nx, -1)
    strip, high2, low2 = pl.pallas_call(
        far_kernel,
        out_shape=[jax.ShapeDtypeStruct((n, LANES), f32) for n in (96, 120, 120)],
        in_specs=[vmem] * 3,
        out_specs=[vmem] * 3,
        compiler_params=grant,
    )(near, left, right)
    strip_b1 = moved(strip, GX, nx, 1)
    strip_a1 = moved(strip, GX, nx, -1)
    below2 = moved(high2, GX, nx, 2)
    above2 = moved(low2, GX, nx, -2)

    powers, gram = pl.pallas_call(
        powers_kernel,
        out_shape=[
            jax.ShapeDtypeStruct((ITERS + 1, NODES, 4 * LANES), f32),
            jax.ShapeDtypeStruct((1, LANES), f32),
        ],
        in_specs=[vmem] * 10,
        out_specs=[vmem] * 2,
        scratch_shapes=[pltpu.VMEM((n, wide), f32) for n in (NODES, NODES, NODES + 32, NODES, 8, 32)],
        compiler_params=grant,
    )(shift, weight, near, below1, above1, below2, above2, strip, strip_b1, strip_a1)
    every = GX + GY
    copies = jnp.broadcast_to(gram, (nx * ny, LANES))
    gathered = lax.all_to_all(copies, every, split_axis=0, concat_axis=0, tiled=True)
    basis, hess, amp = pl.pallas_call(
        functools.partial(combine_kernel, float(NODES * 4 * nx * LANES * ny)),
        out_shape=[
            jax.ShapeDtypeStruct((ITERS + 1, 4 * NODES, LANES), f32),
            jax.ShapeDtypeStruct((ITERS + 1, ITERS), f32),
            jax.ShapeDtypeStruct((1, LANES), f32),
        ],
        in_specs=[vmem] * 3,
        out_specs=[vmem] * 3,
        compiler_params=grant,
    )(shift, powers, gathered)
    return hess, basis, amp[0, 0], raw


def body(source, initial, reaction, stiffness, line_op, face_deriv, wall_flags):
    flat = [v.reshape(4 * NODES, LANES) for v in (source, initial, reaction)]
    hess, basis, amp, raw = fast(*flat, stiffness, line_op, face_deriv, wall_flags.reshape(16, LANES))

    def again(carry):
        raw = lax.optimization_barrier(carry[3])
        initial, source, reaction = raw[0:768].reshape(3, NODES, 4, LANES)
        opened = raw[772:788].reshape(4, 4, LANES)
        line_op, face_deriv = raw[788:796, 0:P_SIZE], raw[796, 0:P_SIZE]
        hess, basis = stepwise(source, initial, reaction, raw[768:772], line_op, face_deriv, opened)
        return jnp.bool_(True), hess, basis.reshape(ITERS + 1, 4 * NODES, LANES), raw

    done = amp <= AMP_LIMIT
    carry = lax.while_loop(lambda carry: jnp.logical_not(carry[0]), again, (done, hess, basis, raw))
    return (carry[1], carry[2].reshape(ITERS + 1, NODES, 4, LANES))


def solution(mesh):
    finer = Mesh(mesh.devices.reshape(4, 2, 4, 8), ("gx_0", "gx_1", "gy_0", "gy_1"))
    placed = (
        P(None, GX, GY),
        P(None, GX, GY),
        P(None, GX, GY),
        P(GX, GY),
        P(),
        P(),
        P(None, GX, GY),
    )
    return jax.shard_map(
        body, mesh=finer, in_specs=placed, out_specs=(P(), P(None, None, GX, GY)), check_vma=False
    )
```

profile of v0, /device:TPU:1, one launch (start us, length us, event | category | flops | bytes accessed | tf_op | source)
XLA Modules:
  0.0 50.6 jit_solution(9711565532445272943)
XLA Ops:
  0.6 1.5 %shard_map.86 = (f32[800,128]{1,0:T(8,128)S(1)}, f32[568,128]{1,0:T(8,128)S(1)}, f32[64,128]{1,0:T(8,128)S(1)}, f32[64,128]{1,0:T(8,128)S(1)}, bf16[96,384]{1,0:T(8,128)(2,1)S(1)}, /*index=5*/f32[8,128]{1,0:T(8,128)S(1)}) custom-call(f32[8,8]{1,0:T(8,128)} %line_in.1, f32[1,8]{1,0:T(1,128)} %bitcast.524, f32[256,128]{1,0:T(8,128)} %bitcast.520, ...), custom_call_target="tpu_custom_call" | custom-call | tf_op jit(solution)/shard_map/pallas_call | solution.py:558
  2.1 3.2 %collective-permute-start.9 = (f32[568,128]{1,0:T(8,128)S(1)}, f32[568,128]{1,0:T(8,128)S(1)}, u32[]{:S(2)}, u32[]{:S(2)}) collective-permute-start(f32[568,128]{1,0:T(8,128)S(1)} %get-tuple-element.522.near), channel_id=1, source_target_pairs={{0,224},{32,0},{64,32},{96,64},{128,96},{160,128},{192,160},{224,1... | collective-permute-start | bytes 872456 | tf_op jit(solution)/shard_map/ppermute | solution.py:555
  5.4 0.0 collective-permute-start.8
  5.4 1.1 %collective-permute-start.10 = (f32[64,128]{1,0:T(8,128)S(1)}, f32[64,128]{1,0:T(8,128)S(1)}, u32[]{:S(2)}, u32[]{:S(2)}) collective-permute-start(f32[64,128]{1,0:T(8,128)S(1)} %get-tuple-element.523), channel_id=1, source_target_pairs={{0,1},{1,2},{2,3},{3,4},{4,5},{5,6},{6,7},{7,8},{8,9},{9,10},{10,1... | collective-permute-start | bytes 98312 | tf_op jit(solution)/shard_map/ppermute | solution.py:555
  6.5 6.1 %collective-permute-start.11 = (f32[64,128]{1,0:T(8,128)S(1)}, f32[64,128]{1,0:T(8,128)S(1)}, u32[]{:S(2)}, u32[]{:S(2)}) collective-permute-start(f32[64,128]{1,0:T(8,128)S(1)} %get-tuple-element.524), channel_id=1, source_target_pairs={{0,31},{1,0},{2,1},{3,2},{4,3},{5,4},{6,5},{7,6},{8,7},{9,8},{10,9... | collective-permute-start | bytes 98312 | tf_op jit(solution)/shard_map/ppermute | solution.py:555
  12.6 1.3 %collective-permute-done.10.left = f32[64,128]{1,0:T(8,128)S(1)} collective-permute-done((f32[64,128]{1,0:T(8,128)S(1)}, f32[64,128]{1,0:T(8,128)S(1)}, u32[]{:S(2)}, u32[]{:S(2)}) %collective-permute-start.10) | collective-permute-done | bytes 32800 | tf_op jit(solution)/shard_map/ppermute | solution.py:555
  13.9 0.0 collective-permute-done.11.right
  13.9 0.1 shard_map.87
  14.0 2.1 %collective-permute-start.15 = (f32[96,128]{1,0:T(8,128)S(1)}, f32[96,128]{1,0:T(8,128)S(1)}, u32[]{:S(2)}, u32[]{:S(2)}) collective-permute-start(f32[96,128]{1,0:T(8,128)S(1)} %get-tuple-element.527.own_strip), channel_id=1, source_target_pairs={{0,224},{32,0},{64,32},{96,64},{128,96},{160,128},{192,160},{224,1... | collective-permute-start | bytes 147464 | tf_op jit(solution)/shard_map/ppermute | solution.py:555
  16.2 0.0 collective-permute-start.12
  16.2 2.7 %collective-permute-start.13 = (f32[120,128]{1,0:T(8,128)S(1)}, f32[120,128]{1,0:T(8,128)S(1)}, u32[]{:S(2)}, u32[]{:S(2)}) collective-permute-start(f32[120,128]{1,0:T(8,128)S(1)} %get-tuple-element.526), channel_id=1, source_target_pairs={{0,192},{32,224},{64,0},{96,32},{128,64},{160,96},{192,128},{224,1... | collective-permute-start | bytes 184328 | tf_op jit(solution)/shard_map/ppermute | solution.py:555
  18.8 0.0 collective-permute-done.15.strip_a1
  18.8 1.0 %collective-permute-start.14 = (f32[96,128]{1,0:T(8,128)S(1)}, f32[96,128]{1,0:T(8,128)S(1)}, u32[]{:S(2)}, u32[]{:S(2)}) collective-permute-start(f32[96,128]{1,0:T(8,128)S(1)} %get-tuple-element.527.own_strip), channel_id=1, source_target_pairs={{0,32},{32,64},{64,96},{96,128},{128,160},{160,192},{192,224},{224... | collective-permute-start | bytes 147464 | tf_op jit(solution)/shard_map/ppermute | solution.py:555
  19.9 2.3 %collective-permute-done.14.strip_b1 = f32[96,128]{1,0:T(8,128)S(1)} collective-permute-done((f32[96,128]{1,0:T(8,128)S(1)}, f32[96,128]{1,0:T(8,128)S(1)}, u32[]{:S(2)}, u32[]{:S(2)}) %collective-permute-start.14) | collective-permute-done | bytes 49184 | tf_op jit(solution)/shard_map/ppermute | solution.py:555
  22.2 0.0 collective-permute-done.12.below2
  22.2 0.0 collective-permute-done.13.above2
  22.2 0.0 collective-permute-done.9.above1
  22.2 0.0 collective-permute-done.8.below1
  22.2 2.6 %shard_map.88 = (f32[6,64,512]{2,1,0:T(8,128)S(1)}, f32[1,128]{1,0:T(1,128)S(1)}) custom-call(f32[8,128]{1,0:T(8,128)S(1)} %get-tuple-element.520.shift_in, bf16[96,384]{1,0:T(8,128)(2,1)S(1)} %get-tuple-element.521.weight, f32[568,128]{1,0:T(8,128)S(1)} %get-tuple-element.522.near, f32[568,128]{1,0:T(8,128)S(1)} %collective-permute-done.8.below1, ...), custom_call_target="tpu_custom_call" | custom-call | tf_op jit(solution)/shard_map/pallas_call | solution.py:588
  24.9 0.1 broadcast_in_dim.114
  24.9 23.9 %all_to_all.53 = f32[256,1,128]{2,1,0:T(1,128)S(1)} all-to-all(f32[256,1,128]{2,1,0:T(1,128)S(1)} %broadcast_in_dim.114), channel_id=1, replica_groups=mesh['gx_0'=4,'gx_1'=2,'gy_0'=4,'gy_1'=8] {'gx_0','gx_1','gy_0','gy_1'}, dimensions={0} | all-to-all | bytes 262144 | tf_op jit(solution)/shard_map/all_to_all | solution.py:601
  48.9 1.3 %shard_map.89 = (f32[6,256,128]{2,1,0:T(8,128)}, f32[6,5]{1,0:T(8,128)}, f32[1,128]{1,0:T(1,128)S(1)}) custom-call(f32[8,128]{1,0:T(8,128)S(1)} %get-tuple-element.520.shift_in, f32[6,64,512]{2,1,0:T(8,128)S(1)} %get-tuple-element.528.powers, f32[256,128]{1,0:T(8,128)S(1)} %bitcast.494), custom_call_target="tpu_custom_call" | custom-call | tf_op jit(solution)/shard_map/pallas_call | solution.py:602
  50.2 0.2 while.41
Async XLA Ops:
  2.1 20.1 %collective-permute-start.9 = (f32[568,128]{1,0:T(8,128)S(1)}, f32[568,128]{1,0:T(8,128)S(1)}, u32[]{:S(2)}, u32[]{:S(2)}) collective-permute-start(f32[568,128]{1,0:T(8,128)S(1)} %get-tuple-element.522.near), channel_id=1, source_target_pairs={{0,224},{32,0},{64,32},{96,64},{128,96},{160,128},{192,160},{224,1... | collective-permute-start | bytes 872456 | tf_op jit(solution)/shard_map/ppermute | solution.py:555
  5.4 16.9 %collective-permute-start.8 = (f32[568,128]{1,0:T(8,128)S(1)}, f32[568,128]{1,0:T(8,128)S(1)}, u32[]{:S(2)}, u32[]{:S(2)}) collective-permute-start(f32[568,128]{1,0:T(8,128)S(1)} %get-tuple-element.522.near), channel_id=1, source_target_pairs={{0,32},{32,64},{64,96},{96,128},{128,160},{160,192},{192,224},{224... | collective-permute-start | bytes 872456 | tf_op jit(solution)/shard_map/ppermute | solution.py:555
  5.4 8.6 %collective-permute-start.10 = (f32[64,128]{1,0:T(8,128)S(1)}, f32[64,128]{1,0:T(8,128)S(1)}, u32[]{:S(2)}, u32[]{:S(2)}) collective-permute-start(f32[64,128]{1,0:T(8,128)S(1)} %get-tuple-element.523), channel_id=1, source_target_pairs={{0,1},{1,2},{2,3},{3,4},{4,5},{5,6},{6,7},{7,8},{8,9},{9,10},{10,1... | collective-permute-start | bytes 98312 | tf_op jit(solution)/shard_map/ppermute | solution.py:555
  6.5 7.4 %collective-permute-start.11 = (f32[64,128]{1,0:T(8,128)S(1)}, f32[64,128]{1,0:T(8,128)S(1)}, u32[]{:S(2)}, u32[]{:S(2)}) collective-permute-start(f32[64,128]{1,0:T(8,128)S(1)} %get-tuple-element.524), channel_id=1, source_target_pairs={{0,31},{1,0},{2,1},{3,2},{4,3},{5,4},{6,5},{7,6},{8,7},{9,8},{10,9... | collective-permute-start | bytes 98312 | tf_op jit(solution)/shard_map/ppermute | solution.py:555
  14.0 4.8 %collective-permute-start.15 = (f32[96,128]{1,0:T(8,128)S(1)}, f32[96,128]{1,0:T(8,128)S(1)}, u32[]{:S(2)}, u32[]{:S(2)}) collective-permute-start(f32[96,128]{1,0:T(8,128)S(1)} %get-tuple-element.527.own_strip), channel_id=1, source_target_pairs={{0,224},{32,0},{64,32},{96,64},{128,96},{160,128},{192,160},{224,1... | collective-permute-start | bytes 147464 | tf_op jit(solution)/shard_map/ppermute | solution.py:555
  16.2 6.1 %collective-permute-start.12 = (f32[120,128]{1,0:T(8,128)S(1)}, f32[120,128]{1,0:T(8,128)S(1)}, u32[]{:S(2)}, u32[]{:S(2)}) collective-permute-start(f32[120,128]{1,0:T(8,128)S(1)} %get-tuple-element.525), channel_id=1, source_target_pairs={{0,64},{32,96},{64,128},{96,160},{128,192},{160,224},{192,0},{224,... | collective-permute-start | bytes 184328 | tf_op jit(solution)/shard_map/ppermute | solution.py:555
  16.2 6.1 %collective-permute-start.13 = (f32[120,128]{1,0:T(8,128)S(1)}, f32[120,128]{1,0:T(8,128)S(1)}, u32[]{:S(2)}, u32[]{:S(2)}) collective-permute-start(f32[120,128]{1,0:T(8,128)S(1)} %get-tuple-element.526), channel_id=1, source_target_pairs={{0,192},{32,224},{64,0},{96,32},{128,64},{160,96},{192,128},{224,1... | collective-permute-start | bytes 184328 | tf_op jit(solution)/shard_map/ppermute | solution.py:555
  18.8 3.4 %collective-permute-start.14 = (f32[96,128]{1,0:T(8,128)S(1)}, f32[96,128]{1,0:T(8,128)S(1)}, u32[]{:S(2)}, u32[]{:S(2)}) collective-permute-start(f32[96,128]{1,0:T(8,128)S(1)} %get-tuple-element.527.own_strip), channel_id=1, source_target_pairs={{0,32},{32,64},{64,96},{96,128},{128,160},{160,192},{192,224},{224... | collective-permute-start | bytes 147464 | tf_op jit(solution)/shard_map/ppermute | solution.py:555
where the time goes:
time: 50.8 us; the launch traced here: 50.6 us
  blocking collectives  23.9 us (47%)
  starting transfers between devices  16.3 us (32%)
  Pallas kernels  5.54 us (11%)
  waiting for transfers between devices  3.64 us (7%)
  between operations  0.9 us (2%)
    all_to_all x1, blocking collectives, fast(): lax.all_to_all(copies, every, split_axis=0, concat_axis=0, tiled=True)  23.9 us
    ppermute x8, starting transfers between devices, moved(): lax.ppermute(value, axis, [(i, (i + by) % size) for i in range(size)])  16.3 us
    ppermute x8, waiting for transfers between devices, moved(): lax.ppermute(value, axis, [(i, (i + by) % size) for i in range(size)])  3.64 us
    pallas_call x1, Pallas kernels, fast(): pl.pallas_call(powers_kernel, out_shape=[jax.ShapeDtypeStruct((ITERS + 1,...  2.63 us
    pallas_call x1, Pallas kernels, fast(): pl.pallas_call(pack_kernel, out_shape=[jax.ShapeDtypeStruct((n, LANES), f...  1.51 us
    pallas_call x1, Pallas kernels, fast(): pl.pallas_call(functools.partial(combine_kernel, float(NODES * 4 * nx * L...  1.32 us
  transfers between devices with their start and end apart: 8, of which 2 were waited for; matrix products, arithmetic and copies ran while one was open for 0% of the time, Pallas kernels for 0%

commit v1 on v0

--- a/solution.py
+++ b/solution.py
@@ -569,8 +569,16 @@
         ],
         compiler_params=grant,
     )(*[pltpu.with_memory_space_constraint(v, pltpu.HBM) for v in held])
-    left = moved(to_up, GY, ny, 1)
-    right = moved(to_down, GY, ny, -1)
+    line = lax.axis_size(GY[1])
+    spot = lax.axis_index(GY[1])
+    first, last = spot == 0, spot == line - 1
+    inside = [(i, i + 1) for i in range(ny) if (i + 1) % line]
+    across = [(i, (i + 1) % ny) for i in range(ny) if (i + 1) % line == 0]
+    left = lax.ppermute(to_up, GY, inside)
+    right = lax.ppermute(to_down, GY, [(b, a) for a, b in inside])
+    swapped = lax.ppermute(jnp.where(last, to_up, to_down), GY, across + [(b, a) for a, b in across])
+    left = jnp.where(first, swapped, left)
+    right = jnp.where(last, swapped, right)
     below1 = moved(near, GX, nx, 1)
     above1 = moved(near, GX, nx, -1)
     strip, high2, low2 = pl.pallas_call(
@@ -580,10 +588,9 @@
         out_specs=[vmem] * 3,
         compiler_params=grant,
     )(near, left, right)
-    strip_b1 = moved(strip, GX, nx, 1)
-    strip_a1 = moved(strip, GX, nx, -1)
     below2 = moved(high2, GX, nx, 2)
     above2 = moved(low2, GX, nx, -2)
+    strips = [moved(strip, GX, nx, by) for by in (1, -1)]
 
     powers, gram = pl.pallas_call(
         powers_kernel,
@@ -595,7 +602,7 @@
         out_specs=[vmem] * 2,
         scratch_shapes=[pltpu.VMEM((n, wide), f32) for n in (NODES, NODES, NODES + 32, NODES, 8, 32)],
         compiler_params=grant,
-    )(shift, weight, near, below1, above1, below2, above2, strip, strip_b1, strip_a1)
+    )(shift, weight, near, below1, above1, below2, above2, strip, *strips)
     every = GX + GY
     copies = jnp.broadcast_to(gram, (nx * ny, LANES))
     gathered = lax.all_to_all(copies, every, split_axis=0, concat_axis=0, tiled=True)

time: 50.8 us -> 53.6 us (1.055)
  starting transfers between devices: 16.3 us -> 20.2 us
  blocking collectives: 23.9 us -> 22.7 us
    ppermute x0 -> x3, starting transfers between devices: none -> 13.1 us  [the longest x1 10.5 us: fast(): lax.ppermute(jnp.where(last, to_up, to_down), GY, across + [(b, a) for a,...]
    ppermute x8 -> x6, starting transfers between devices: 16.3 us -> 7.08 us  [moved(): lax.ppermute(value, axis, [(i, (i + by) % size) for i in range(size)])]
    all_to_all x1, blocking collectives: 23.9 us -> 22.7 us  [fast(): lax.all_to_all(copies, every, split_axis=0, concat_axis=0, tiled=True)]
    ppermute x0 -> x3, waiting for transfers between devices: none -> 1.18 us  [the longest x1 1.17 us: fast(): right = lax.ppermute(to_down, GY, [(b, a) for a, b in inside])]
    ppermute x8 -> x6, waiting for transfers between devices: 3.64 us -> 2.5 us  [moved(): lax.ppermute(value, axis, [(i, (i + by) % size) for i in range(size)])]
  transfers between devices with their start and end apart: 8 -> 9, of which waited for: 2 -> 3; matrix products, arithmetic and copies ran while one was open for 0% -> 0% of each run, Pallas kernels for 0% -> 0%
where the time goes in v1:
time: 53.6 us; the launch traced here: 53.4 us
  blocking collectives  22.7 us (42%)
  starting transfers between devices  20.2 us (38%)
  Pallas kernels  5.52 us (10%)
  waiting for transfers between devices  3.68 us (7%)
  between operations  0.94 us (2%)
    all_to_all x1, blocking collectives, fast(): lax.all_to_all(copies, every, split_axis=0, concat_axis=0, tiled=True)  22.7 us
    ppermute x1, starting transfers between devices, fast(): lax.ppermute(jnp.where(last, to_up, to_down), GY, across + [(b, a) for a,...  10.5 us
    ppermute x6, starting transfers between devices, moved(): lax.ppermute(value, axis, [(i, (i + by) % size) for i in range(size)])  7.08 us
    pallas_call x1, Pallas kernels, fast(): pl.pallas_call(powers_kernel, out_shape=[jax.ShapeDtypeStruct((ITERS + 1,...  2.62 us
    ppermute x6, waiting for transfers between devices, moved(): lax.ppermute(value, axis, [(i, (i + by) % size) for i in range(size)])  2.5 us
    pallas_call x1, Pallas kernels, fast(): pl.pallas_call(pack_kernel, out_shape=[jax.ShapeDtypeStruct((n, LANES), f...  1.5 us
    pallas_call x1, Pallas kernels, fast(): pl.pallas_call(functools.partial(combine_kernel, float(NODES * 4 * nx * L...  1.32 us
    ppermute x1, starting transfers between devices, fast(): right = lax.ppermute(to_down, GY, [(b, a) for a, b in inside])  1.29 us
  transfers between devices with their start and end apart: 9, of which 3 were waited for; matrix products, arithmetic and copies ran while one was open for 0% of the time, Pallas kernels for 0%

profile of v1, /device:TPU:1, one launch (start us, length us, event | category | flops | bytes accessed | tf_op | source)
XLA Modules:
  0.0 53.4 jit_solution(12915924975165129696)
XLA Ops:
  0.6 1.5 %shard_map.86 = (f32[800,128]{1,0:T(8,128)S(1)}, f32[568,128]{1,0:T(8,128)S(1)}, f32[64,128]{1,0:T(8,128)S(1)}, f32[64,128]{1,0:T(8,128)S(1)}, bf16[96,384]{1,0:T(8,128)(2,1)S(1)}, /*index=5*/f32[8,128]{1,0:T(8,128)S(1)}) custom-call(f32[8,8]{1,0:T(8,128)} %line_in.1, f32[1,8]{1,0:T(1,128)} %bitcast.524, f32[256,128]{1,0:T(8,128)} %bitcast.520, ...), custom_call_target="tpu_custom_call" | custom-call | tf_op jit(solution)/shard_map/pallas_call | solution.py:558
  2.2 10.5 %collective-permute-start.10 = (f32[64,128]{1,0:T(8,128)S(1)}, f32[64,128]{1,0:T(8,128)S(1)}, u32[]{:S(2)}, u32[]{:S(2)}) collective-permute-start(f32[64,128]{1,0:T(8,128)S(1)} %broadcast_select_fusion.1), channel_id=1, source_target_pairs={{7,8},{15,16},{23,24},{31,0},{8,7},{16,15},{24,23},{0,31},{39,40},... | collective-permute-start | bytes 98312 | tf_op jit(solution)/shard_map/ppermute | solution.py:579
  12.7 1.3 %collective-permute-start.11 = (f32[64,128]{1,0:T(8,128)S(1)}, f32[64,128]{1,0:T(8,128)S(1)}, u32[]{:S(2)}, u32[]{:S(2)}) collective-permute-start(f32[64,128]{1,0:T(8,128)S(1)} %get-tuple-element.523), channel_id=1, source_target_pairs={{0,1},{1,2},{2,3},{3,4},{4,5},{5,6},{6,7},{8,9},{9,10},{10,11},{11... | collective-permute-start | bytes 98312 | tf_op jit(solution)/shard_map/ppermute | solution.py:577
  14.0 1.3 %collective-permute-start.12 = (f32[64,128]{1,0:T(8,128)S(1)}, f32[64,128]{1,0:T(8,128)S(1)}, u32[]{:S(2)}, u32[]{:S(2)}) collective-permute-start(f32[64,128]{1,0:T(8,128)S(1)} %get-tuple-element.524), channel_id=1, source_target_pairs={{1,0},{2,1},{3,2},{4,3},{5,4},{6,5},{7,6},{9,8},{10,9},{11,10},{12... | collective-permute-start | bytes 98312 | tf_op jit(solution)/shard_map/ppermute | solution.py:578
  15.3 1.0 %collective-permute-start.9 = (f32[568,128]{1,0:T(8,128)S(1)}, f32[568,128]{1,0:T(8,128)S(1)}, u32[]{:S(2)}, u32[]{:S(2)}) collective-permute-start(f32[568,128]{1,0:T(8,128)S(1)} %get-tuple-element.522.near), channel_id=1, source_target_pairs={{0,224},{32,0},{64,32},{96,64},{128,96},{160,128},{192,160},{224,1... | collective-permute-start | bytes 872456 | tf_op jit(solution)/shard_map/ppermute | solution.py:555
  16.2 1.2 %collective-permute-start.8 = (f32[568,128]{1,0:T(8,128)S(1)}, f32[568,128]{1,0:T(8,128)S(1)}, u32[]{:S(2)}, u32[]{:S(2)}) collective-permute-start(f32[568,128]{1,0:T(8,128)S(1)} %get-tuple-element.522.near), channel_id=1, source_target_pairs={{0,32},{32,64},{64,96},{96,128},{128,160},{160,192},{192,224},{224... | collective-permute-start | bytes 872456 | tf_op jit(solution)/shard_map/ppermute | solution.py:555
  17.4 0.0 collective-permute-done.10
  17.5 0.0 collective-permute-done.11
  17.5 1.2 %collective-permute-done.12 = f32[64,128]{1,0:T(8,128)S(1)} collective-permute-done((f32[64,128]{1,0:T(8,128)S(1)}, f32[64,128]{1,0:T(8,128)S(1)}, u32[]{:S(2)}, u32[]{:S(2)}) %collective-permute-start.12) | collective-permute-done | bytes 32800 | tf_op jit(solution)/shard_map/ppermute | solution.py:578
  18.6 0.1 shard_map.87
  18.7 2.1 %collective-permute-start.16 = (f32[96,128]{1,0:T(8,128)S(1)}, f32[96,128]{1,0:T(8,128)S(1)}, u32[]{:S(2)}, u32[]{:S(2)}) collective-permute-start(f32[96,128]{1,0:T(8,128)S(1)} %get-tuple-element.527.own_strip), channel_id=1, source_target_pairs={{0,224},{32,0},{64,32},{96,64},{128,96},{160,128},{192,160},{224,1... | collective-permute-start | bytes 147464 | tf_op jit(solution)/shard_map/ppermute | solution.py:555
  20.8 1.3 %collective-permute-start.13 = (f32[120,128]{1,0:T(8,128)S(1)}, f32[120,128]{1,0:T(8,128)S(1)}, u32[]{:S(2)}, u32[]{:S(2)}) collective-permute-start(f32[120,128]{1,0:T(8,128)S(1)} %get-tuple-element.525), channel_id=1, source_target_pairs={{0,64},{32,96},{64,128},{96,160},{128,192},{160,224},{192,0},{224,... | collective-permute-start | bytes 184328 | tf_op jit(solution)/shard_map/ppermute | solution.py:555
  22.1 1.4 %collective-permute-start.14 = (f32[120,128]{1,0:T(8,128)S(1)}, f32[120,128]{1,0:T(8,128)S(1)}, u32[]{:S(2)}, u32[]{:S(2)}) collective-permute-start(f32[120,128]{1,0:T(8,128)S(1)} %get-tuple-element.526), channel_id=1, source_target_pairs={{0,192},{32,224},{64,0},{96,32},{128,64},{160,96},{192,128},{224,1... | collective-permute-start | bytes 184328 | tf_op jit(solution)/shard_map/ppermute | solution.py:555
  23.6 0.5 collective-permute-done.16.strip_a1
  24.1 0.1 collective-permute-start.15
  24.2 2.0 %collective-permute-done.15.strip_b1 = f32[96,128]{1,0:T(8,128)S(1)} collective-permute-done((f32[96,128]{1,0:T(8,128)S(1)}, f32[96,128]{1,0:T(8,128)S(1)}, u32[]{:S(2)}, u32[]{:S(2)}) %collective-permute-start.15) | collective-permute-done | bytes 49184 | tf_op jit(solution)/shard_map/ppermute | solution.py:555
  26.1 0.0 collective-permute-done.13.below2
  26.1 0.0 collective-permute-done.14.above2
  26.1 0.0 collective-permute-done.9.above1
  26.1 0.0 collective-permute-done.8.below1
  26.2 2.6 %shard_map.88 = (f32[6,64,512]{2,1,0:T(8,128)S(1)}, f32[1,128]{1,0:T(1,128)S(1)}) custom-call(f32[8,128]{1,0:T(8,128)S(1)} %get-tuple-element.520.shift_in, bf16[96,384]{1,0:T(8,128)(2,1)S(1)} %get-tuple-element.521.weight, f32[568,128]{1,0:T(8,128)S(1)} %get-tuple-element.522.near, f32[568,128]{1,0:T(8,128)S(1)} %collective-permute-done.8.below1, ...), custom_call_target="tpu_custom_call" | custom-call | tf_op jit(solution)/shard_map/pallas_call | solution.py:595
  28.8 0.1 broadcast_in_dim.114
  28.9 22.7 %all_to_all.53 = f32[256,1,128]{2,1,0:T(1,128)S(1)} all-to-all(f32[256,1,128]{2,1,0:T(1,128)S(1)} %broadcast_in_dim.114), channel_id=1, replica_groups=mesh['gx_0'=4,'gx_1'=2,'gy_0'=4,'gy_1'=8] {'gx_0','gx_1','gy_0','gy_1'}, dimensions={0} | all-to-all | bytes 262144 | tf_op jit(solution)/shard_map/all_to_all | solution.py:608
  51.6 1.3 %shard_map.89 = (f32[6,256,128]{2,1,0:T(8,128)}, f32[6,5]{1,0:T(8,128)}, f32[1,128]{1,0:T(1,128)S(1)}) custom-call(f32[8,128]{1,0:T(8,128)S(1)} %get-tuple-element.520.shift_in, f32[6,64,512]{2,1,0:T(8,128)S(1)} %get-tuple-element.528.powers, f32[256,128]{1,0:T(8,128)S(1)} %bitcast.494), custom_call_target="tpu_custom_call" | custom-call | tf_op jit(solution)/shard_map/pallas_call | solution.py:609
  53.0 0.2 while.41
  (2 shorter events, 0.0 us)
Async XLA Ops:
  2.2 15.3 %collective-permute-start.10 = (f32[64,128]{1,0:T(8,128)S(1)}, f32[64,128]{1,0:T(8,128)S(1)}, u32[]{:S(2)}, u32[]{:S(2)}) collective-permute-start(f32[64,128]{1,0:T(8,128)S(1)} %broadcast_select_fusion.1), channel_id=1, source_target_pairs={{7,8},{15,16},{23,24},{31,0},{8,7},{16,15},{24,23},{0,31},{39,40},... | collective-permute-start | bytes 98312 | tf_op jit(solution)/shard_map/ppermute | solution.py:579
  12.7 4.8 %collective-permute-start.11 = (f32[64,128]{1,0:T(8,128)S(1)}, f32[64,128]{1,0:T(8,128)S(1)}, u32[]{:S(2)}, u32[]{:S(2)}) collective-permute-start(f32[64,128]{1,0:T(8,128)S(1)} %get-tuple-element.523), channel_id=1, source_target_pairs={{0,1},{1,2},{2,3},{3,4},{4,5},{5,6},{6,7},{8,9},{9,10},{10,11},{11... | collective-permute-start | bytes 98312 | tf_op jit(solution)/shard_map/ppermute | solution.py:577
  14.0 4.7 %collective-permute-start.12 = (f32[64,128]{1,0:T(8,128)S(1)}, f32[64,128]{1,0:T(8,128)S(1)}, u32[]{:S(2)}, u32[]{:S(2)}) collective-permute-start(f32[64,128]{1,0:T(8,128)S(1)} %get-tuple-element.524), channel_id=1, source_target_pairs={{1,0},{2,1},{3,2},{4,3},{5,4},{6,5},{7,6},{9,8},{10,9},{11,10},{12... | collective-permute-start | bytes 98312 | tf_op jit(solution)/shard_map/ppermute | solution.py:578
  15.3 10.9 %collective-permute-start.9 = (f32[568,128]{1,0:T(8,128)S(1)}, f32[568,128]{1,0:T(8,128)S(1)}, u32[]{:S(2)}, u32[]{:S(2)}) collective-permute-start(f32[568,128]{1,0:T(8,128)S(1)} %get-tuple-element.522.near), channel_id=1, source_target_pairs={{0,224},{32,0},{64,32},{96,64},{128,96},{160,128},{192,160},{224,1... | collective-permute-start | bytes 872456 | tf_op jit(solution)/shard_map/ppermute | solution.py:555
  16.2 9.9 %collective-permute-start.8 = (f32[568,128]{1,0:T(8,128)S(1)}, f32[568,128]{1,0:T(8,128)S(1)}, u32[]{:S(2)}, u32[]{:S(2)}) collective-permute-start(f32[568,128]{1,0:T(8,128)S(1)} %get-tuple-element.522.near), channel_id=1, source_target_pairs={{0,32},{32,64},{64,96},{96,128},{128,160},{160,192},{192,224},{224... | collective-permute-start | bytes 872456 | tf_op jit(solution)/shard_map/ppermute | solution.py:555
  18.7 5.4 %collective-permute-start.16 = (f32[96,128]{1,0:T(8,128)S(1)}, f32[96,128]{1,0:T(8,128)S(1)}, u32[]{:S(2)}, u32[]{:S(2)}) collective-permute-start(f32[96,128]{1,0:T(8,128)S(1)} %get-tuple-element.527.own_strip), channel_id=1, source_target_pairs={{0,224},{32,0},{64,32},{96,64},{128,96},{160,128},{192,160},{224,1... | collective-permute-start | bytes 147464 | tf_op jit(solution)/shard_map/ppermute | solution.py:555
  20.8 5.3 %collective-permute-start.13 = (f32[120,128]{1,0:T(8,128)S(1)}, f32[120,128]{1,0:T(8,128)S(1)}, u32[]{:S(2)}, u32[]{:S(2)}) collective-permute-start(f32[120,128]{1,0:T(8,128)S(1)} %get-tuple-element.525), channel_id=1, source_target_pairs={{0,64},{32,96},{64,128},{96,160},{128,192},{160,224},{192,0},{224,... | collective-permute-start | bytes 184328 | tf_op jit(solution)/shard_map/ppermute | solution.py:555
  22.1 4.0 %collective-permute-start.14 = (f32[120,128]{1,0:T(8,128)S(1)}, f32[120,128]{1,0:T(8,128)S(1)}, u32[]{:S(2)}, u32[]{:S(2)}) collective-permute-start(f32[120,128]{1,0:T(8,128)S(1)} %get-tuple-element.526), channel_id=1, source_target_pairs={{0,192},{32,224},{64,0},{96,32},{128,64},{160,96},{192,128},{224,1... | collective-permute-start | bytes 184328 | tf_op jit(solution)/shard_map/ppermute | solution.py:555
  24.1 2.0 %collective-permute-start.15 = (f32[96,128]{1,0:T(8,128)S(1)}, f32[96,128]{1,0:T(8,128)S(1)}, u32[]{:S(2)}, u32[]{:S(2)}) collective-permute-start(f32[96,128]{1,0:T(8,128)S(1)} %get-tuple-element.527.own_strip), channel_id=1, source_target_pairs={{0,32},{32,64},{64,96},{96,128},{128,160},{160,192},{192,224},{224... | collective-permute-start | bytes 147464 | tf_op jit(solution)/shard_map/ppermute | solution.py:555

commit v2 on v1

--- a/solution.py
+++ b/solution.py
@@ -572,11 +572,12 @@
     line = lax.axis_size(GY[1])
     spot = lax.axis_index(GY[1])
     first, last = spot == 0, spot == line - 1
-    inside = [(i, i + 1) for i in range(ny) if (i + 1) % line]
+    inside = [(i, i + 1 if (i + 1) % line else i + 1 - line) for i in range(ny)]
     across = [(i, (i + 1) % ny) for i in range(ny) if (i + 1) % line == 0]
+    still = [(i, i) for i in range(ny) if i % line not in (0, line - 1)]
     left = lax.ppermute(to_up, GY, inside)
     right = lax.ppermute(to_down, GY, [(b, a) for a, b in inside])
-    swapped = lax.ppermute(jnp.where(last, to_up, to_down), GY, across + [(b, a) for a, b in across])
+    swapped = lax.ppermute(jnp.where(last, to_up, to_down), GY, across + [(b, a) for a, b in across] + still)
     left = jnp.where(first, swapped, left)
     right = jnp.where(last, swapped, right)
     below1 = moved(near, GX, nx, 1)

time: 53.6 us -> 52.2 us (0.974)
  blocking collectives: 22.7 us -> 21.3 us
  waiting for transfers between devices: 3.68 us -> 4.56 us
  starting transfers between devices: 20.2 us -> 19.4 us
    ppermute x6, waiting for transfers between devices: 2.5 us -> 4.55 us  [moved(): lax.ppermute(value, axis, [(i, (i + by) % size) for i in range(size)])]
    all_to_all x1, blocking collectives: 22.7 us -> 21.3 us  [fast(): lax.all_to_all(copies, every, split_axis=0, concat_axis=0, tiled=True)]
    ppermute x1, starting transfers between devices: 1.29 us -> 2.66 us  [fast(): right = lax.ppermute(to_down, GY, [(b, a) for a, b in inside])]
    ppermute x1, starting transfers between devices: 1.29 us -> 0.08 us  [fast(): left = lax.ppermute(to_up, GY, inside)]
    ppermute x1, waiting for transfers between devices: 1.17 us -> 0.01 us  [fast(): right = lax.ppermute(to_down, GY, [(b, a) for a, b in inside])]
    ppermute x6, starting transfers between devices: 7.08 us -> 6.14 us  [moved(): lax.ppermute(value, axis, [(i, (i + by) % size) for i in range(size)])]
where the time goes in v2:
time: 52.2 us; the launch traced here: 52 us
  blocking collectives  21.3 us (41%)
  starting transfers between devices  19.4 us (37%)
  Pallas kernels  5.52 us (11%)
  waiting for transfers between devices  4.56 us (9%)
  between operations  0.93 us (2%)
    all_to_all x1, blocking collectives, fast(): lax.all_to_all(copies, every, split_axis=0, concat_axis=0, tiled=True)  21.3 us
    ppermute x1, starting transfers between devices, fast(): lax.ppermute(jnp.where(last, to_up, to_down), GY, across + [(b, a) for a,...  10.5 us
    ppermute x6, starting transfers between devices, moved(): lax.ppermute(value, axis, [(i, (i + by) % size) for i in range(size)])  6.14 us
    ppermute x6, waiting for transfers between devices, moved(): lax.ppermute(value, axis, [(i, (i + by) % size) for i in range(size)])  4.55 us
    ppermute x1, starting transfers between devices, fast(): right = lax.ppermute(to_down, GY, [(b, a) for a, b in inside])  2.66 us
    pallas_call x1, Pallas kernels, fast(): pl.pallas_call(powers_kernel, out_shape=[jax.ShapeDtypeStruct((ITERS + 1,...  2.62 us
    pallas_call x1, Pallas kernels, fast(): pl.pallas_call(pack_kernel, out_shape=[jax.ShapeDtypeStruct((n, LANES), f...  1.5 us
    pallas_call x1, Pallas kernels, fast(): pl.pallas_call(functools.partial(combine_kernel, float(NODES * 4 * nx * L...  1.32 us
  transfers between devices with their start and end apart: 9, of which 3 were waited for; matrix products, arithmetic and copies ran while one was open for 0% of the time, Pallas kernels for 0%

profile of v2, /device:TPU:1, one launch (start us, length us, event | category | flops | bytes accessed | tf_op | source)
XLA Modules:
  0.0 52.0 jit_solution(11428088663934587254)
XLA Ops:
  0.6 1.5 %shard_map.86 = (f32[800,128]{1,0:T(8,128)S(1)}, f32[568,128]{1,0:T(8,128)S(1)}, f32[64,128]{1,0:T(8,128)S(1)}, f32[64,128]{1,0:T(8,128)S(1)}, bf16[96,384]{1,0:T(8,128)(2,1)S(1)}, /*index=5*/f32[8,128]{1,0:T(8,128)S(1)}) custom-call(f32[8,8]{1,0:T(8,128)} %line_in.1, f32[1,8]{1,0:T(1,128)} %bitcast.524, f32[256,128]{1,0:T(8,128)} %bitcast.520, ...), custom_call_target="tpu_custom_call" | custom-call | tf_op jit(solution)/shard_map/pallas_call | solution.py:558
  2.2 10.5 %collective-permute-start.10 = (f32[64,128]{1,0:T(8,128)S(1)}, f32[64,128]{1,0:T(8,128)S(1)}, u32[]{:S(2)}, u32[]{:S(2)}) collective-permute-start(f32[64,128]{1,0:T(8,128)S(1)} %broadcast_select_fusion.1), channel_id=1, source_target_pairs={{7,8},{15,16},{23,24},{31,0},{8,7},{16,15},{24,23},{0,31},{1,1},{2... | collective-permute-start | bytes 98312 | tf_op jit(solution)/shard_map/ppermute | solution.py:580
  12.7 0.1 collective-permute-start.11
  12.8 2.7 %collective-permute-start.12 = (f32[64,128]{1,0:T(8,128)S(1)}, f32[64,128]{1,0:T(8,128)S(1)}, u32[]{:S(2)}, u32[]{:S(2)}) collective-permute-start(f32[64,128]{1,0:T(8,128)S(1)} %get-tuple-element.524), channel_id=1, source_target_pairs={{1,0},{2,1},{3,2},{4,3},{5,4},{6,5},{7,6},{0,7},{9,8},{10,9},{11,1... | collective-permute-start | bytes 98312 | tf_op jit(solution)/shard_map/ppermute | solution.py:579
  15.4 1.5 %collective-permute-start.9 = (f32[568,128]{1,0:T(8,128)S(1)}, f32[568,128]{1,0:T(8,128)S(1)}, u32[]{:S(2)}, u32[]{:S(2)}) collective-permute-start(f32[568,128]{1,0:T(8,128)S(1)} %get-tuple-element.522.near), channel_id=1, source_target_pairs={{0,224},{32,0},{64,32},{96,64},{128,96},{160,128},{192,160},{224,1... | collective-permute-start | bytes 872456 | tf_op jit(solution)/shard_map/ppermute | solution.py:555
  16.9 1.2 %collective-permute-start.8 = (f32[568,128]{1,0:T(8,128)S(1)}, f32[568,128]{1,0:T(8,128)S(1)}, u32[]{:S(2)}, u32[]{:S(2)}) collective-permute-start(f32[568,128]{1,0:T(8,128)S(1)} %get-tuple-element.522.near), channel_id=1, source_target_pairs={{0,32},{32,64},{64,96},{96,128},{128,160},{160,192},{192,224},{224... | collective-permute-start | bytes 872456 | tf_op jit(solution)/shard_map/ppermute | solution.py:555
  18.1 0.0 collective-permute-done.10
  18.1 0.0 collective-permute-done.11
  18.1 0.0 collective-permute-done.12
  18.2 0.1 shard_map.87
  18.2 0.7 %collective-permute-start.16 = (f32[96,128]{1,0:T(8,128)S(1)}, f32[96,128]{1,0:T(8,128)S(1)}, u32[]{:S(2)}, u32[]{:S(2)}) collective-permute-start(f32[96,128]{1,0:T(8,128)S(1)} %get-tuple-element.527.own_strip), channel_id=1, source_target_pairs={{0,224},{32,0},{64,32},{96,64},{128,96},{160,128},{192,160},{224,1... | collective-permute-start | bytes 147464 | tf_op jit(solution)/shard_map/ppermute | solution.py:555
  18.9 1.3 %collective-permute-start.13 = (f32[120,128]{1,0:T(8,128)S(1)}, f32[120,128]{1,0:T(8,128)S(1)}, u32[]{:S(2)}, u32[]{:S(2)}) collective-permute-start(f32[120,128]{1,0:T(8,128)S(1)} %get-tuple-element.525), channel_id=1, source_target_pairs={{0,64},{32,96},{64,128},{96,160},{128,192},{160,224},{192,0},{224,... | collective-permute-start | bytes 184328 | tf_op jit(solution)/shard_map/ppermute | solution.py:555
  20.2 1.4 %collective-permute-start.14 = (f32[120,128]{1,0:T(8,128)S(1)}, f32[120,128]{1,0:T(8,128)S(1)}, u32[]{:S(2)}, u32[]{:S(2)}) collective-permute-start(f32[120,128]{1,0:T(8,128)S(1)} %get-tuple-element.526), channel_id=1, source_target_pairs={{0,192},{32,224},{64,0},{96,32},{128,64},{160,96},{192,128},{224,1... | collective-permute-start | bytes 184328 | tf_op jit(solution)/shard_map/ppermute | solution.py:555
  21.7 2.0 %collective-permute-done.16.strip_a1 = f32[96,128]{1,0:T(8,128)S(1)} collective-permute-done((f32[96,128]{1,0:T(8,128)S(1)}, f32[96,128]{1,0:T(8,128)S(1)}, u32[]{:S(2)}, u32[]{:S(2)}) %collective-permute-start.16) | collective-permute-done | bytes 49184 | tf_op jit(solution)/shard_map/ppermute | solution.py:555
  23.7 0.0 collective-permute-start.15
  23.7 2.0 %collective-permute-done.15.strip_b1 = f32[96,128]{1,0:T(8,128)S(1)} collective-permute-done((f32[96,128]{1,0:T(8,128)S(1)}, f32[96,128]{1,0:T(8,128)S(1)}, u32[]{:S(2)}, u32[]{:S(2)}) %collective-permute-start.15) | collective-permute-done | bytes 49184 | tf_op jit(solution)/shard_map/ppermute | solution.py:555
  25.6 0.6 %collective-permute-done.13.below2 = f32[120,128]{1,0:T(8,128)S(1)} collective-permute-done((f32[120,128]{1,0:T(8,128)S(1)}, f32[120,128]{1,0:T(8,128)S(1)}, u32[]{:S(2)}, u32[]{:S(2)}) %collective-permute-start.13) | collective-permute-done | bytes 61472 | tf_op jit(solution)/shard_map/ppermute | solution.py:555
  26.2 0.0 collective-permute-done.14.above2
  26.2 0.0 collective-permute-done.9.above1
  26.2 0.0 collective-permute-done.8.below1
  26.3 2.6 %shard_map.88 = (f32[6,64,512]{2,1,0:T(8,128)S(1)}, f32[1,128]{1,0:T(1,128)S(1)}) custom-call(f32[8,128]{1,0:T(8,128)S(1)} %get-tuple-element.520.shift_in, bf16[96,384]{1,0:T(8,128)(2,1)S(1)} %get-tuple-element.521.weight, f32[568,128]{1,0:T(8,128)S(1)} %get-tuple-element.522.near, f32[568,128]{1,0:T(8,128)S(1)} %collective-permute-done.8.below1, ...), custom_call_target="tpu_custom_call" | custom-call | tf_op jit(solution)/shard_map/pallas_call | solution.py:596
  28.9 0.1 broadcast_in_dim.114
  28.9 21.3 %all_to_all.53 = f32[256,1,128]{2,1,0:T(1,128)S(1)} all-to-all(f32[256,1,128]{2,1,0:T(1,128)S(1)} %broadcast_in_dim.114), channel_id=1, replica_groups=mesh['gx_0'=4,'gx_1'=2,'gy_0'=4,'gy_1'=8] {'gx_0','gx_1','gy_0','gy_1'}, dimensions={0} | all-to-all | bytes 262144 | tf_op jit(solution)/shard_map/all_to_all | solution.py:609
  50.2 1.3 %shard_map.89 = (f32[6,256,128]{2,1,0:T(8,128)}, f32[6,5]{1,0:T(8,128)}, f32[1,128]{1,0:T(1,128)S(1)}) custom-call(f32[8,128]{1,0:T(8,128)S(1)} %get-tuple-element.520.shift_in, f32[6,64,512]{2,1,0:T(8,128)S(1)} %get-tuple-element.528.powers, f32[256,128]{1,0:T(8,128)S(1)} %bitcast.494), custom_call_target="tpu_custom_call" | custom-call | tf_op jit(solution)/shard_map/pallas_call | solution.py:610
  51.6 0.2 while.41
  (2 shorter events, 0.0 us)
Async XLA Ops:
  2.2 16.0 %collective-permute-start.10 = (f32[64,128]{1,0:T(8,128)S(1)}, f32[64,128]{1,0:T(8,128)S(1)}, u32[]{:S(2)}, u32[]{:S(2)}) collective-permute-start(f32[64,128]{1,0:T(8,128)S(1)} %broadcast_select_fusion.1), channel_id=1, source_target_pairs={{7,8},{15,16},{23,24},{31,0},{8,7},{16,15},{24,23},{0,31},{1,1},{2... | collective-permute-start | bytes 98312 | tf_op jit(solution)/shard_map/ppermute | solution.py:580
  12.7 5.5 %collective-permute-start.11 = (f32[64,128]{1,0:T(8,128)S(1)}, f32[64,128]{1,0:T(8,128)S(1)}, u32[]{:S(2)}, u32[]{:S(2)}) collective-permute-start(f32[64,128]{1,0:T(8,128)S(1)} %get-tuple-element.523), channel_id=1, source_target_pairs={{0,1},{1,2},{2,3},{3,4},{4,5},{5,6},{6,7},{7,0},{8,9},{9,10},{10,1... | collective-permute-start | bytes 98312 | tf_op jit(solution)/shard_map/ppermute | solution.py:578
  12.8 5.4 %collective-permute-start.12 = (f32[64,128]{1,0:T(8,128)S(1)}, f32[64,128]{1,0:T(8,128)S(1)}, u32[]{:S(2)}, u32[]{:S(2)}) collective-permute-start(f32[64,128]{1,0:T(8,128)S(1)} %get-tuple-element.524), channel_id=1, source_target_pairs={{1,0},{2,1},{3,2},{4,3},{5,4},{6,5},{7,6},{0,7},{9,8},{10,9},{11,1... | collective-permute-start | bytes 98312 | tf_op jit(solution)/shard_map/ppermute | solution.py:579
  15.4 10.8 %collective-permute-start.9 = (f32[568,128]{1,0:T(8,128)S(1)}, f32[568,128]{1,0:T(8,128)S(1)}, u32[]{:S(2)}, u32[]{:S(2)}) collective-permute-start(f32[568,128]{1,0:T(8,128)S(1)} %get-tuple-element.522.near), channel_id=1, source_target_pairs={{0,224},{32,0},{64,32},{96,64},{128,96},{160,128},{192,160},{224,1... | collective-permute-start | bytes 872456 | tf_op jit(solution)/shard_map/ppermute | solution.py:555
  16.9 9.3 %collective-permute-start.8 = (f32[568,128]{1,0:T(8,128)S(1)}, f32[568,128]{1,0:T(8,128)S(1)}, u32[]{:S(2)}, u32[]{:S(2)}) collective-permute-start(f32[568,128]{1,0:T(8,128)S(1)} %get-tuple-element.522.near), channel_id=1, source_target_pairs={{0,32},{32,64},{64,96},{96,128},{128,160},{160,192},{192,224},{224... | collective-permute-start | bytes 872456 | tf_op jit(solution)/shard_map/ppermute | solution.py:555
  18.2 5.4 %collective-permute-start.16 = (f32[96,128]{1,0:T(8,128)S(1)}, f32[96,128]{1,0:T(8,128)S(1)}, u32[]{:S(2)}, u32[]{:S(2)}) collective-permute-start(f32[96,128]{1,0:T(8,128)S(1)} %get-tuple-element.527.own_strip), channel_id=1, source_target_pairs={{0,224},{32,0},{64,32},{96,64},{128,96},{160,128},{192,160},{224,1... | collective-permute-start | bytes 147464 | tf_op jit(solution)/shard_map/ppermute | solution.py:555
  18.9 7.3 %collective-permute-start.13 = (f32[120,128]{1,0:T(8,128)S(1)}, f32[120,128]{1,0:T(8,128)S(1)}, u32[]{:S(2)}, u32[]{:S(2)}) collective-permute-start(f32[120,128]{1,0:T(8,128)S(1)} %get-tuple-element.525), channel_id=1, source_target_pairs={{0,64},{32,96},{64,128},{96,160},{128,192},{160,224},{192,0},{224,... | collective-permute-start | bytes 184328 | tf_op jit(solution)/shard_map/ppermute | solution.py:555
  20.2 6.0 %collective-permute-start.14 = (f32[120,128]{1,0:T(8,128)S(1)}, f32[120,128]{1,0:T(8,128)S(1)}, u32[]{:S(2)}, u32[]{:S(2)}) collective-permute-start(f32[120,128]{1,0:T(8,128)S(1)} %get-tuple-element.526), channel_id=1, source_target_pairs={{0,192},{32,224},{64,0},{96,32},{128,64},{160,96},{192,128},{224,1... | collective-permute-start | bytes 184328 | tf_op jit(solution)/shard_map/ppermute | solution.py:555
  23.7 2.0 %collective-permute-start.15 = (f32[96,128]{1,0:T(8,128)S(1)}, f32[96,128]{1,0:T(8,128)S(1)}, u32[]{:S(2)}, u32[]{:S(2)}) collective-permute-start(f32[96,128]{1,0:T(8,128)S(1)} %get-tuple-element.527.own_strip), channel_id=1, source_target_pairs={{0,32},{32,64},{64,96},{96,128},{128,160},{160,192},{192,224},{224... | collective-permute-start | bytes 147464 | tf_op jit(solution)/shard_map/ppermute | solution.py:555

commit v3 on v0

--- a/solution.py
+++ b/solution.py
@@ -580,10 +580,9 @@
         out_specs=[vmem] * 3,
         compiler_params=grant,
     )(near, left, right)
-    strip_b1 = moved(strip, GX, nx, 1)
-    strip_a1 = moved(strip, GX, nx, -1)
     below2 = moved(high2, GX, nx, 2)
     above2 = moved(low2, GX, nx, -2)
+    strips = [moved(strip, GX, nx, by) for by in (1, -1)]
 
     powers, gram = pl.pallas_call(
         powers_kernel,
@@ -595,7 +594,7 @@
         out_specs=[vmem] * 2,
         scratch_shapes=[pltpu.VMEM((n, wide), f32) for n in (NODES, NODES, NODES + 32, NODES, 8, 32)],
         compiler_params=grant,
-    )(shift, weight, near, below1, above1, below2, above2, strip, strip_b1, strip_a1)
+    )(shift, weight, near, below1, above1, below2, above2, strip, *strips)
     every = GX + GY
     copies = jnp.broadcast_to(gram, (nx * ny, LANES))
     gathered = lax.all_to_all(copies, every, split_axis=0, concat_axis=0, tiled=True)

time: 50.8 us -> 50.8 us (level)
  no operation moved by 1% of the time
where the time goes in v3:
time: 50.8 us; the launch traced here: 50.6 us
  blocking collectives  23.9 us (47%)
  starting transfers between devices  16.3 us (32%)
  Pallas kernels  5.54 us (11%)
  waiting for transfers between devices  3.64 us (7%)
  between operations  0.9 us (2%)
    all_to_all x1, blocking collectives, fast(): lax.all_to_all(copies, every, split_axis=0, concat_axis=0, tiled=True)  23.9 us
    ppermute x8, starting transfers between devices, moved(): lax.ppermute(value, axis, [(i, (i + by) % size) for i in range(size)])  16.3 us
    ppermute x8, waiting for transfers between devices, moved(): lax.ppermute(value, axis, [(i, (i + by) % size) for i in range(size)])  3.64 us
    pallas_call x1, Pallas kernels, fast(): pl.pallas_call(powers_kernel, out_shape=[jax.ShapeDtypeStruct((ITERS + 1,...  2.63 us
    pallas_call x1, Pallas kernels, fast(): pl.pallas_call(pack_kernel, out_shape=[jax.ShapeDtypeStruct((n, LANES), f...  1.51 us
    pallas_call x1, Pallas kernels, fast(): pl.pallas_call(functools.partial(combine_kernel, float(NODES * 4 * nx * L...  1.32 us
  transfers between devices with their start and end apart: 8, of which 2 were waited for; matrix products, arithmetic and copies ran while one was open for 0% of the time, Pallas kernels for 0%

profile of v3, /device:TPU:1, one launch (start us, length us, event | category | flops | bytes accessed | tf_op | source)
XLA Modules:
  0.0 50.6 jit_solution(9711565532445272943)
XLA Ops:
  0.6 1.5 %shard_map.86 = (f32[800,128]{1,0:T(8,128)S(1)}, f32[568,128]{1,0:T(8,128)S(1)}, f32[64,128]{1,0:T(8,128)S(1)}, f32[64,128]{1,0:T(8,128)S(1)}, bf16[96,384]{1,0:T(8,128)(2,1)S(1)}, /*index=5*/f32[8,128]{1,0:T(8,128)S(1)}) custom-call(f32[8,8]{1,0:T(8,128)} %line_in.1, f32[1,8]{1,0:T(1,128)} %bitcast.524, f32[256,128]{1,0:T(8,128)} %bitcast.520, ...), custom_call_target="tpu_custom_call" | custom-call | tf_op jit(solution)/shard_map/pallas_call | solution.py:558
  2.1 3.2 %collective-permute-start.9 = (f32[568,128]{1,0:T(8,128)S(1)}, f32[568,128]{1,0:T(8,128)S(1)}, u32[]{:S(2)}, u32[]{:S(2)}) collective-permute-start(f32[568,128]{1,0:T(8,128)S(1)} %get-tuple-element.522.near), channel_id=1, source_target_pairs={{0,224},{32,0},{64,32},{96,64},{128,96},{160,128},{192,160},{224,1... | collective-permute-start | bytes 872456 | tf_op jit(solution)/shard_map/ppermute | solution.py:555
  5.4 0.0 collective-permute-start.8
  5.4 1.1 %collective-permute-start.10 = (f32[64,128]{1,0:T(8,128)S(1)}, f32[64,128]{1,0:T(8,128)S(1)}, u32[]{:S(2)}, u32[]{:S(2)}) collective-permute-start(f32[64,128]{1,0:T(8,128)S(1)} %get-tuple-element.523), channel_id=1, source_target_pairs={{0,1},{1,2},{2,3},{3,4},{4,5},{5,6},{6,7},{7,8},{8,9},{9,10},{10,1... | collective-permute-start | bytes 98312 | tf_op jit(solution)/shard_map/ppermute | solution.py:555
  6.5 6.1 %collective-permute-start.11 = (f32[64,128]{1,0:T(8,128)S(1)}, f32[64,128]{1,0:T(8,128)S(1)}, u32[]{:S(2)}, u32[]{:S(2)}) collective-permute-start(f32[64,128]{1,0:T(8,128)S(1)} %get-tuple-element.524), channel_id=1, source_target_pairs={{0,31},{1,0},{2,1},{3,2},{4,3},{5,4},{6,5},{7,6},{8,7},{9,8},{10,9... | collective-permute-start | bytes 98312 | tf_op jit(solution)/shard_map/ppermute | solution.py:555
  12.6 1.3 %collective-permute-done.10.left = f32[64,128]{1,0:T(8,128)S(1)} collective-permute-done((f32[64,128]{1,0:T(8,128)S(1)}, f32[64,128]{1,0:T(8,128)S(1)}, u32[]{:S(2)}, u32[]{:S(2)}) %collective-permute-start.10) | collective-permute-done | bytes 32800 | tf_op jit(solution)/shard_map/ppermute | solution.py:555
  13.9 0.0 collective-permute-done.11.right
  13.9 0.1 shard_map.87
  14.0 2.1 %collective-permute-start.15 = (f32[96,128]{1,0:T(8,128)S(1)}, f32[96,128]{1,0:T(8,128)S(1)}, u32[]{:S(2)}, u32[]{:S(2)}) collective-permute-start(f32[96,128]{1,0:T(8,128)S(1)} %get-tuple-element.527.own_strip), channel_id=1, source_target_pairs={{0,224},{32,0},{64,32},{96,64},{128,96},{160,128},{192,160},{224,1... | collective-permute-start | bytes 147464 | tf_op jit(solution)/shard_map/ppermute | solution.py:555
  16.2 0.0 collective-permute-start.12
  16.2 2.7 %collective-permute-start.13 = (f32[120,128]{1,0:T(8,128)S(1)}, f32[120,128]{1,0:T(8,128)S(1)}, u32[]{:S(2)}, u32[]{:S(2)}) collective-permute-start(f32[120,128]{1,0:T(8,128)S(1)} %get-tuple-element.526), channel_id=1, source_target_pairs={{0,192},{32,224},{64,0},{96,32},{128,64},{160,96},{192,128},{224,1... | collective-permute-start | bytes 184328 | tf_op jit(solution)/shard_map/ppermute | solution.py:555
  18.8 0.0 collective-permute-done.15.strip_a1
  18.8 1.0 %collective-permute-start.14 = (f32[96,128]{1,0:T(8,128)S(1)}, f32[96,128]{1,0:T(8,128)S(1)}, u32[]{:S(2)}, u32[]{:S(2)}) collective-permute-start(f32[96,128]{1,0:T(8,128)S(1)} %get-tuple-element.527.own_strip), channel_id=1, source_target_pairs={{0,32},{32,64},{64,96},{96,128},{128,160},{160,192},{192,224},{224... | collective-permute-start | bytes 147464 | tf_op jit(solution)/shard_map/ppermute | solution.py:555
  19.9 2.3 %collective-permute-done.14.strip_b1 = f32[96,128]{1,0:T(8,128)S(1)} collective-permute-done((f32[96,128]{1,0:T(8,128)S(1)}, f32[96,128]{1,0:T(8,128)S(1)}, u32[]{:S(2)}, u32[]{:S(2)}) %collective-permute-start.14) | collective-permute-done | bytes 49184 | tf_op jit(solution)/shard_map/ppermute | solution.py:555
  22.2 0.0 collective-permute-done.12.below2
  22.2 0.0 collective-permute-done.13.above2
  22.2 0.0 collective-permute-done.9.above1
  22.2 0.0 collective-permute-done.8.below1
  22.2 2.6 %shard_map.88 = (f32[6,64,512]{2,1,0:T(8,128)S(1)}, f32[1,128]{1,0:T(1,128)S(1)}) custom-call(f32[8,128]{1,0:T(8,128)S(1)} %get-tuple-element.520.shift_in, bf16[96,384]{1,0:T(8,128)(2,1)S(1)} %get-tuple-element.521.weight, f32[568,128]{1,0:T(8,128)S(1)} %get-tuple-element.522.near, f32[568,128]{1,0:T(8,128)S(1)} %collective-permute-done.8.below1, ...), custom_call_target="tpu_custom_call" | custom-call | tf_op jit(solution)/shard_map/pallas_call | solution.py:587
  24.9 0.1 broadcast_in_dim.114
  24.9 23.9 %all_to_all.53 = f32[256,1,128]{2,1,0:T(1,128)S(1)} all-to-all(f32[256,1,128]{2,1,0:T(1,128)S(1)} %broadcast_in_dim.114), channel_id=1, replica_groups=mesh['gx_0'=4,'gx_1'=2,'gy_0'=4,'gy_1'=8] {'gx_0','gx_1','gy_0','gy_1'}, dimensions={0} | all-to-all | bytes 262144 | tf_op jit(solution)/shard_map/all_to_all | solution.py:600
  48.9 1.3 %shard_map.89 = (f32[6,256,128]{2,1,0:T(8,128)}, f32[6,5]{1,0:T(8,128)}, f32[1,128]{1,0:T(1,128)S(1)}) custom-call(f32[8,128]{1,0:T(8,128)S(1)} %get-tuple-element.520.shift_in, f32[6,64,512]{2,1,0:T(8,128)S(1)} %get-tuple-element.528.powers, f32[256,128]{1,0:T(8,128)S(1)} %bitcast.494), custom_call_target="tpu_custom_call" | custom-call | tf_op jit(solution)/shard_map/pallas_call | solution.py:601
  50.2 0.2 while.41
Async XLA Ops:
  2.1 20.1 %collective-permute-start.9 = (f32[568,128]{1,0:T(8,128)S(1)}, f32[568,128]{1,0:T(8,128)S(1)}, u32[]{:S(2)}, u32[]{:S(2)}) collective-permute-start(f32[568,128]{1,0:T(8,128)S(1)} %get-tuple-element.522.near), channel_id=1, source_target_pairs={{0,224},{32,0},{64,32},{96,64},{128,96},{160,128},{192,160},{224,1... | collective-permute-start | bytes 872456 | tf_op jit(solution)/shard_map/ppermute | solution.py:555
  5.4 16.9 %collective-permute-start.8 = (f32[568,128]{1,0:T(8,128)S(1)}, f32[568,128]{1,0:T(8,128)S(1)}, u32[]{:S(2)}, u32[]{:S(2)}) collective-permute-start(f32[568,128]{1,0:T(8,128)S(1)} %get-tuple-element.522.near), channel_id=1, source_target_pairs={{0,32},{32,64},{64,96},{96,128},{128,160},{160,192},{192,224},{224... | collective-permute-start | bytes 872456 | tf_op jit(solution)/shard_map/ppermute | solution.py:555
  5.4 8.6 %collective-permute-start.10 = (f32[64,128]{1,0:T(8,128)S(1)}, f32[64,128]{1,0:T(8,128)S(1)}, u32[]{:S(2)}, u32[]{:S(2)}) collective-permute-start(f32[64,128]{1,0:T(8,128)S(1)} %get-tuple-element.523), channel_id=1, source_target_pairs={{0,1},{1,2},{2,3},{3,4},{4,5},{5,6},{6,7},{7,8},{8,9},{9,10},{10,1... | collective-permute-start | bytes 98312 | tf_op jit(solution)/shard_map/ppermute | solution.py:555
  6.5 7.4 %collective-permute-start.11 = (f32[64,128]{1,0:T(8,128)S(1)}, f32[64,128]{1,0:T(8,128)S(1)}, u32[]{:S(2)}, u32[]{:S(2)}) collective-permute-start(f32[64,128]{1,0:T(8,128)S(1)} %get-tuple-element.524), channel_id=1, source_target_pairs={{0,31},{1,0},{2,1},{3,2},{4,3},{5,4},{6,5},{7,6},{8,7},{9,8},{10,9... | collective-permute-start | bytes 98312 | tf_op jit(solution)/shard_map/ppermute | solution.py:555
  14.0 4.8 %collective-permute-start.15 = (f32[96,128]{1,0:T(8,128)S(1)}, f32[96,128]{1,0:T(8,128)S(1)}, u32[]{:S(2)}, u32[]{:S(2)}) collective-permute-start(f32[96,128]{1,0:T(8,128)S(1)} %get-tuple-element.527.own_strip), channel_id=1, source_target_pairs={{0,224},{32,0},{64,32},{96,64},{128,96},{160,128},{192,160},{224,1... | collective-permute-start | bytes 147464 | tf_op jit(solution)/shard_map/ppermute | solution.py:555
  16.2 6.1 %collective-permute-start.12 = (f32[120,128]{1,0:T(8,128)S(1)}, f32[120,128]{1,0:T(8,128)S(1)}, u32[]{:S(2)}, u32[]{:S(2)}) collective-permute-start(f32[120,128]{1,0:T(8,128)S(1)} %get-tuple-element.525), channel_id=1, source_target_pairs={{0,64},{32,96},{64,128},{96,160},{128,192},{160,224},{192,0},{224,... | collective-permute-start | bytes 184328 | tf_op jit(solution)/shard_map/ppermute | solution.py:555
  16.2 6.1 %collective-permute-start.13 = (f32[120,128]{1,0:T(8,128)S(1)}, f32[120,128]{1,0:T(8,128)S(1)}, u32[]{:S(2)}, u32[]{:S(2)}) collective-permute-start(f32[120,128]{1,0:T(8,128)S(1)} %get-tuple-element.526), channel_id=1, source_target_pairs={{0,192},{32,224},{64,0},{96,32},{128,64},{160,96},{192,128},{224,1... | collective-permute-start | bytes 184328 | tf_op jit(solution)/shard_map/ppermute | solution.py:555
  18.8 3.4 %collective-permute-start.14 = (f32[96,128]{1,0:T(8,128)S(1)}, f32[96,128]{1,0:T(8,128)S(1)}, u32[]{:S(2)}, u32[]{:S(2)}) collective-permute-start(f32[96,128]{1,0:T(8,128)S(1)} %get-tuple-element.527.own_strip), channel_id=1, source_target_pairs={{0,32},{32,64},{64,96},{96,128},{128,160},{160,192},{192,224},{224... | collective-permute-start | bytes 147464 | tf_op jit(solution)/shard_map/ppermute | solution.py:555

commit v4 on v3

--- a/solution.py
+++ b/solution.py
@@ -327,13 +327,14 @@
     edge = jnp.where((lanes >= 64) & (lanes < 96), turned(left[0:32, :], -32), edge)
     edge = jnp.where(lanes >= 96, right[0:32, :], edge)
     strip[64:96, :] = edge
-    for out, close, face in ((high2, 3, LAST_EAST), (low2, 0, FIRST_WEST)):
+    facing = (edge[8:32], jnp.concatenate([edge[0:8], edge[16:32]], axis=0))
+    for out, close, face, corner in ((high2, 3, LAST_EAST, facing[0]), (low2, 0, FIRST_WEST, facing[1])):
         block = BLOCK * close
         out[0:64, :] = near[block : block + 64, :]
         out[64:72, :] = near[block + THICK : block + BLOCK, :]
         out[72:80, :] = near[face : face + 8, :]
         out[80:88, :] = near[ENDS : ENDS + 8, :]
-        out[88:120, :] = edge
+        out[88:112, :] = corner
 
 
 def powers_kernel(
@@ -376,8 +377,11 @@
                 part = turned(ref[top : top + count, :], target - zero)
                 value = jnp.where((ids >= start) & (ids < stop), part, value)
             if count == 32:
-                value = jnp.where(ids < 16, turned(below2[88:120, :], -16 - 32 * side), value)
-                value = jnp.where(ids >= 112, turned(above2[88:120, :], 112 - 32 * side), value)
+                blank = jnp.zeros((8, LANES), jnp.float32)
+                corner = jnp.concatenate([blank, below2[88:112, :]], axis=0)
+                value = jnp.where(ids < 16, turned(corner, -16 - 32 * side), value)
+                corner = jnp.concatenate([above2[88:96, :], blank, above2[96:112, :]], axis=0)
+                value = jnp.where(ids >= 112, turned(corner, 112 - 32 * side), value)
             made.append(value)
         put(ROWS + side, made[1], made[3][0:1], [made[3][1 + f : 2 + f] for f in range(4)])
         local[ROWS + side] = functools.partial(lambda value, a: value[8 * a : 8 * a + 8], made[0])
@@ -575,7 +579,7 @@
     above1 = moved(near, GX, nx, -1)
     strip, high2, low2 = pl.pallas_call(
         far_kernel,
-        out_shape=[jax.ShapeDtypeStruct((n, LANES), f32) for n in (96, 120, 120)],
+        out_shape=[jax.ShapeDtypeStruct((n, LANES), f32) for n in (96, 112, 112)],
         in_specs=[vmem] * 3,
         out_specs=[vmem] * 3,
         compiler_params=grant,

time: 50.8 us -> 50.7 us (level)
  no operation moved by 1% of the time
where the time goes in v4:
time: 50.7 us; the launch traced here: 50.6 us
  blocking collectives  23.9 us (47%)
  starting transfers between devices  16.3 us (32%)
  Pallas kernels  5.5 us (11%)
  waiting for transfers between devices  3.64 us (7%)
  between operations  0.9 us (2%)
    all_to_all x1, blocking collectives, fast(): lax.all_to_all(copies, every, split_axis=0, concat_axis=0, tiled=True)  23.9 us
    ppermute x8, starting transfers between devices, moved(): lax.ppermute(value, axis, [(i, (i + by) % size) for i in range(size)])  16.3 us
    ppermute x8, waiting for transfers between devices, moved(): lax.ppermute(value, axis, [(i, (i + by) % size) for i in range(size)])  3.64 us
    pallas_call x1, Pallas kernels, fast(): pl.pallas_call(powers_kernel, out_shape=[jax.ShapeDtypeStruct((ITERS + 1,...  2.6 us
    pallas_call x1, Pallas kernels, fast(): pl.pallas_call(pack_kernel, out_shape=[jax.ShapeDtypeStruct((n, LANES), f...  1.51 us
    pallas_call x1, Pallas kernels, fast(): pl.pallas_call(functools.partial(combine_kernel, float(NODES * 4 * nx * L...  1.3 us
  transfers between devices with their start and end apart: 8, of which 2 were waited for; matrix products, arithmetic and copies ran while one was open for 0% of the time, Pallas kernels for 0%

profile of v4, /device:TPU:1, one launch (start us, length us, event | category | flops | bytes accessed | tf_op | source)
XLA Modules:
  0.0 50.6 jit_solution(1130245740613733748)
XLA Ops:
  0.6 1.5 %shard_map.86 = (f32[800,128]{1,0:T(8,128)S(1)}, f32[568,128]{1,0:T(8,128)S(1)}, f32[64,128]{1,0:T(8,128)S(1)}, f32[64,128]{1,0:T(8,128)S(1)}, bf16[96,384]{1,0:T(8,128)(2,1)S(1)}, /*index=5*/f32[8,128]{1,0:T(8,128)S(1)}) custom-call(f32[8,8]{1,0:T(8,128)} %line_in.1, f32[1,8]{1,0:T(1,128)} %bitcast.524, f32[256,128]{1,0:T(8,128)} %bitcast.520, ...), custom_call_target="tpu_custom_call" | custom-call | tf_op jit(solution)/shard_map/pallas_call | solution.py:562
  2.1 3.2 %collective-permute-start.9 = (f32[568,128]{1,0:T(8,128)S(1)}, f32[568,128]{1,0:T(8,128)S(1)}, u32[]{:S(2)}, u32[]{:S(2)}) collective-permute-start(f32[568,128]{1,0:T(8,128)S(1)} %get-tuple-element.522.near), channel_id=1, source_target_pairs={{0,224},{32,0},{64,32},{96,64},{128,96},{160,128},{192,160},{224,1... | collective-permute-start | bytes 872456 | tf_op jit(solution)/shard_map/ppermute | solution.py:559
  5.4 0.0 collective-permute-start.8
  5.4 1.1 %collective-permute-start.10 = (f32[64,128]{1,0:T(8,128)S(1)}, f32[64,128]{1,0:T(8,128)S(1)}, u32[]{:S(2)}, u32[]{:S(2)}) collective-permute-start(f32[64,128]{1,0:T(8,128)S(1)} %get-tuple-element.523), channel_id=1, source_target_pairs={{0,1},{1,2},{2,3},{3,4},{4,5},{5,6},{6,7},{7,8},{8,9},{9,10},{10,1... | collective-permute-start | bytes 98312 | tf_op jit(solution)/shard_map/ppermute | solution.py:559
  6.5 6.1 %collective-permute-start.11 = (f32[64,128]{1,0:T(8,128)S(1)}, f32[64,128]{1,0:T(8,128)S(1)}, u32[]{:S(2)}, u32[]{:S(2)}) collective-permute-start(f32[64,128]{1,0:T(8,128)S(1)} %get-tuple-element.524), channel_id=1, source_target_pairs={{0,31},{1,0},{2,1},{3,2},{4,3},{5,4},{6,5},{7,6},{8,7},{9,8},{10,9... | collective-permute-start | bytes 98312 | tf_op jit(solution)/shard_map/ppermute | solution.py:559
  12.6 1.3 %collective-permute-done.10.left = f32[64,128]{1,0:T(8,128)S(1)} collective-permute-done((f32[64,128]{1,0:T(8,128)S(1)}, f32[64,128]{1,0:T(8,128)S(1)}, u32[]{:S(2)}, u32[]{:S(2)}) %collective-permute-start.10) | collective-permute-done | bytes 32800 | tf_op jit(solution)/shard_map/ppermute | solution.py:559
  13.9 0.0 collective-permute-done.11.right
  13.9 0.1 shard_map.87
  14.0 2.1 %collective-permute-start.15 = (f32[96,128]{1,0:T(8,128)S(1)}, f32[96,128]{1,0:T(8,128)S(1)}, u32[]{:S(2)}, u32[]{:S(2)}) collective-permute-start(f32[96,128]{1,0:T(8,128)S(1)} %get-tuple-element.527.own_strip), channel_id=1, source_target_pairs={{0,224},{32,0},{64,32},{96,64},{128,96},{160,128},{192,160},{224,1... | collective-permute-start | bytes 147464 | tf_op jit(solution)/shard_map/ppermute | solution.py:559
  16.2 0.0 collective-permute-start.12
  16.2 2.7 %collective-permute-start.13 = (f32[112,128]{1,0:T(8,128)S(1)}, f32[112,128]{1,0:T(8,128)S(1)}, u32[]{:S(2)}, u32[]{:S(2)}) collective-permute-start(f32[112,128]{1,0:T(8,128)S(1)} %get-tuple-element.526), channel_id=1, source_target_pairs={{0,192},{32,224},{64,0},{96,32},{128,64},{160,96},{192,128},{224,1... | collective-permute-start | bytes 172040 | tf_op jit(solution)/shard_map/ppermute | solution.py:559
  18.8 0.0 collective-permute-done.15.strip_a1
  18.8 1.0 %collective-permute-start.14 = (f32[96,128]{1,0:T(8,128)S(1)}, f32[96,128]{1,0:T(8,128)S(1)}, u32[]{:S(2)}, u32[]{:S(2)}) collective-permute-start(f32[96,128]{1,0:T(8,128)S(1)} %get-tuple-element.527.own_strip), channel_id=1, source_target_pairs={{0,32},{32,64},{64,96},{96,128},{128,160},{160,192},{192,224},{224... | collective-permute-start | bytes 147464 | tf_op jit(solution)/shard_map/ppermute | solution.py:559
  19.9 2.3 %collective-permute-done.14.strip_b1 = f32[96,128]{1,0:T(8,128)S(1)} collective-permute-done((f32[96,128]{1,0:T(8,128)S(1)}, f32[96,128]{1,0:T(8,128)S(1)}, u32[]{:S(2)}, u32[]{:S(2)}) %collective-permute-start.14) | collective-permute-done | bytes 49184 | tf_op jit(solution)/shard_map/ppermute | solution.py:559
  22.2 0.0 collective-permute-done.12.below2
  22.2 0.0 collective-permute-done.13.above2
  22.2 0.0 collective-permute-done.9.above1
  22.2 0.0 collective-permute-done.8.below1
  22.2 2.6 %shard_map.88 = (f32[6,64,512]{2,1,0:T(8,128)S(1)}, f32[1,128]{1,0:T(1,128)S(1)}) custom-call(f32[8,128]{1,0:T(8,128)S(1)} %get-tuple-element.520.shift_in, bf16[96,384]{1,0:T(8,128)(2,1)S(1)} %get-tuple-element.521.weight, f32[568,128]{1,0:T(8,128)S(1)} %get-tuple-element.522.near, f32[568,128]{1,0:T(8,128)S(1)} %collective-permute-done.8.below1, ...), custom_call_target="tpu_custom_call" | custom-call | tf_op jit(solution)/shard_map/pallas_call | solution.py:591
  24.8 0.1 broadcast_in_dim.114
  24.9 23.9 %all_to_all.53 = f32[256,1,128]{2,1,0:T(1,128)S(1)} all-to-all(f32[256,1,128]{2,1,0:T(1,128)S(1)} %broadcast_in_dim.114), channel_id=1, replica_groups=mesh['gx_0'=4,'gx_1'=2,'gy_0'=4,'gy_1'=8] {'gx_0','gx_1','gy_0','gy_1'}, dimensions={0} | all-to-all | bytes 262144 | tf_op jit(solution)/shard_map/all_to_all | solution.py:604
  48.8 1.3 %shard_map.89 = (f32[6,256,128]{2,1,0:T(8,128)}, f32[6,5]{1,0:T(8,128)}, f32[1,128]{1,0:T(1,128)S(1)}) custom-call(f32[8,128]{1,0:T(8,128)S(1)} %get-tuple-element.520.shift_in, f32[6,64,512]{2,1,0:T(8,128)S(1)} %get-tuple-element.528.powers, f32[256,128]{1,0:T(8,128)S(1)} %bitcast.494), custom_call_target="tpu_custom_call" | custom-call | tf_op jit(solution)/shard_map/pallas_call | solution.py:605
  50.1 0.2 while.41
Async XLA Ops:
  2.1 20.1 %collective-permute-start.9 = (f32[568,128]{1,0:T(8,128)S(1)}, f32[568,128]{1,0:T(8,128)S(1)}, u32[]{:S(2)}, u32[]{:S(2)}) collective-permute-start(f32[568,128]{1,0:T(8,128)S(1)} %get-tuple-element.522.near), channel_id=1, source_target_pairs={{0,224},{32,0},{64,32},{96,64},{128,96},{160,128},{192,160},{224,1... | collective-permute-start | bytes 872456 | tf_op jit(solution)/shard_map/ppermute | solution.py:559
  5.4 16.9 %collective-permute-start.8 = (f32[568,128]{1,0:T(8,128)S(1)}, f32[568,128]{1,0:T(8,128)S(1)}, u32[]{:S(2)}, u32[]{:S(2)}) collective-permute-start(f32[568,128]{1,0:T(8,128)S(1)} %get-tuple-element.522.near), channel_id=1, source_target_pairs={{0,32},{32,64},{64,96},{96,128},{128,160},{160,192},{192,224},{224... | collective-permute-start | bytes 872456 | tf_op jit(solution)/shard_map/ppermute | solution.py:559
  5.4 8.6 %collective-permute-start.10 = (f32[64,128]{1,0:T(8,128)S(1)}, f32[64,128]{1,0:T(8,128)S(1)}, u32[]{:S(2)}, u32[]{:S(2)}) collective-permute-start(f32[64,128]{1,0:T(8,128)S(1)} %get-tuple-element.523), channel_id=1, source_target_pairs={{0,1},{1,2},{2,3},{3,4},{4,5},{5,6},{6,7},{7,8},{8,9},{9,10},{10,1... | collective-permute-start | bytes 98312 | tf_op jit(solution)/shard_map/ppermute | solution.py:559
  6.5 7.4 %collective-permute-start.11 = (f32[64,128]{1,0:T(8,128)S(1)}, f32[64,128]{1,0:T(8,128)S(1)}, u32[]{:S(2)}, u32[]{:S(2)}) collective-permute-start(f32[64,128]{1,0:T(8,128)S(1)} %get-tuple-element.524), channel_id=1, source_target_pairs={{0,31},{1,0},{2,1},{3,2},{4,3},{5,4},{6,5},{7,6},{8,7},{9,8},{10,9... | collective-permute-start | bytes 98312 | tf_op jit(solution)/shard_map/ppermute | solution.py:559
  14.0 4.8 %collective-permute-start.15 = (f32[96,128]{1,0:T(8,128)S(1)}, f32[96,128]{1,0:T(8,128)S(1)}, u32[]{:S(2)}, u32[]{:S(2)}) collective-permute-start(f32[96,128]{1,0:T(8,128)S(1)} %get-tuple-element.527.own_strip), channel_id=1, source_target_pairs={{0,224},{32,0},{64,32},{96,64},{128,96},{160,128},{192,160},{224,1... | collective-permute-start | bytes 147464 | tf_op jit(solution)/shard_map/ppermute | solution.py:559
  16.2 6.1 %collective-permute-start.12 = (f32[112,128]{1,0:T(8,128)S(1)}, f32[112,128]{1,0:T(8,128)S(1)}, u32[]{:S(2)}, u32[]{:S(2)}) collective-permute-start(f32[112,128]{1,0:T(8,128)S(1)} %get-tuple-element.525), channel_id=1, source_target_pairs={{0,64},{32,96},{64,128},{96,160},{128,192},{160,224},{192,0},{224,... | collective-permute-start | bytes 172040 | tf_op jit(solution)/shard_map/ppermute | solution.py:559
  16.2 6.1 %collective-permute-start.13 = (f32[112,128]{1,0:T(8,128)S(1)}, f32[112,128]{1,0:T(8,128)S(1)}, u32[]{:S(2)}, u32[]{:S(2)}) collective-permute-start(f32[112,128]{1,0:T(8,128)S(1)} %get-tuple-element.526), channel_id=1, source_target_pairs={{0,192},{32,224},{64,0},{96,32},{128,64},{160,96},{192,128},{224,1... | collective-permute-start | bytes 172040 | tf_op jit(solution)/shard_map/ppermute | solution.py:559
  18.8 3.4 %collective-permute-start.14 = (f32[96,128]{1,0:T(8,128)S(1)}, f32[96,128]{1,0:T(8,128)S(1)}, u32[]{:S(2)}, u32[]{:S(2)}) collective-permute-start(f32[96,128]{1,0:T(8,128)S(1)} %get-tuple-element.527.own_strip), channel_id=1, source_target_pairs={{0,32},{32,64},{64,96},{96,128},{128,160},{160,192},{192,224},{224... | collective-permute-start | bytes 147464 | tf_op jit(solution)/shard_map/ppermute | solution.py:559

commit v5 on v4

--- a/solution.py
+++ b/solution.py
@@ -586,7 +586,8 @@
     )(near, left, right)
     below2 = moved(high2, GX, nx, 2)
     above2 = moved(low2, GX, nx, -2)
-    strips = [moved(strip, GX, nx, by) for by in (1, -1)]
+    strip_b1 = moved(strip, GX, nx, 1)
+    strip_a1 = moved(strip, GX, nx, -1)
 
     powers, gram = pl.pallas_call(
         powers_kernel,
@@ -598,7 +599,7 @@
         out_specs=[vmem] * 2,
         scratch_shapes=[pltpu.VMEM((n, wide), f32) for n in (NODES, NODES, NODES + 32, NODES, 8, 32)],
         compiler_params=grant,
-    )(shift, weight, near, below1, above1, below2, above2, strip, *strips)
+    )(shift, weight, near, below1, above1, below2, above2, strip, strip_b1, strip_a1)
     every = GX + GY
     copies = jnp.broadcast_to(gram, (nx * ny, LANES))
     gathered = lax.all_to_all(copies, every, split_axis=0, concat_axis=0, tiled=True)

time: 50.7 us -> 50.7 us (level)
  no operation moved by 1% of the time
where the time goes in v5:
time: 50.7 us; the launch traced here: 50.6 us
  blocking collectives  23.9 us (47%)
  starting transfers between devices  16.3 us (32%)
  Pallas kernels  5.5 us (11%)
  waiting for transfers between devices  3.64 us (7%)
  between operations  0.9 us (2%)
    all_to_all x1, blocking collectives, fast(): lax.all_to_all(copies, every, split_axis=0, concat_axis=0, tiled=True)  23.9 us
    ppermute x8, starting transfers between devices, moved(): lax.ppermute(value, axis, [(i, (i + by) % size) for i in range(size)])  16.3 us
    ppermute x8, waiting for transfers between devices, moved(): lax.ppermute(value, axis, [(i, (i + by) % size) for i in range(size)])  3.64 us
    pallas_call x1, Pallas kernels, fast(): pl.pallas_call(powers_kernel, out_shape=[jax.ShapeDtypeStruct((ITERS + 1,...  2.6 us
    pallas_call x1, Pallas kernels, fast(): pl.pallas_call(pack_kernel, out_shape=[jax.ShapeDtypeStruct((n, LANES), f...  1.51 us
    pallas_call x1, Pallas kernels, fast(): pl.pallas_call(functools.partial(combine_kernel, float(NODES * 4 * nx * L...  1.3 us
  transfers between devices with their start and end apart: 8, of which 2 were waited for; matrix products, arithmetic and copies ran while one was open for 0% of the time, Pallas kernels for 0%

profile of v5, /device:TPU:1, one launch (start us, length us, event | category | flops | bytes accessed | tf_op | source)
XLA Modules:
  0.0 50.6 jit_solution(1130245740613733748)
XLA Ops:
  0.6 1.5 %shard_map.86 = (f32[800,128]{1,0:T(8,128)S(1)}, f32[568,128]{1,0:T(8,128)S(1)}, f32[64,128]{1,0:T(8,128)S(1)}, f32[64,128]{1,0:T(8,128)S(1)}, bf16[96,384]{1,0:T(8,128)(2,1)S(1)}, /*index=5*/f32[8,128]{1,0:T(8,128)S(1)}) custom-call(f32[8,8]{1,0:T(8,128)} %line_in.1, f32[1,8]{1,0:T(1,128)} %bitcast.524, f32[256,128]{1,0:T(8,128)} %bitcast.520, ...), custom_call_target="tpu_custom_call" | custom-call | tf_op jit(solution)/shard_map/pallas_call | solution.py:562
  2.1 3.2 %collective-permute-start.9 = (f32[568,128]{1,0:T(8,128)S(1)}, f32[568,128]{1,0:T(8,128)S(1)}, u32[]{:S(2)}, u32[]{:S(2)}) collective-permute-start(f32[568,128]{1,0:T(8,128)S(1)} %get-tuple-element.522.near), channel_id=1, source_target_pairs={{0,224},{32,0},{64,32},{96,64},{128,96},{160,128},{192,160},{224,1... | collective-permute-start | bytes 872456 | tf_op jit(solution)/shard_map/ppermute | solution.py:559
  5.4 0.0 collective-permute-start.8
  5.4 1.1 %collective-permute-start.10 = (f32[64,128]{1,0:T(8,128)S(1)}, f32[64,128]{1,0:T(8,128)S(1)}, u32[]{:S(2)}, u32[]{:S(2)}) collective-permute-start(f32[64,128]{1,0:T(8,128)S(1)} %get-tuple-element.523), channel_id=1, source_target_pairs={{0,1},{1,2},{2,3},{3,4},{4,5},{5,6},{6,7},{7,8},{8,9},{9,10},{10,1... | collective-permute-start | bytes 98312 | tf_op jit(solution)/shard_map/ppermute | solution.py:559
  6.5 6.1 %collective-permute-start.11 = (f32[64,128]{1,0:T(8,128)S(1)}, f32[64,128]{1,0:T(8,128)S(1)}, u32[]{:S(2)}, u32[]{:S(2)}) collective-permute-start(f32[64,128]{1,0:T(8,128)S(1)} %get-tuple-element.524), channel_id=1, source_target_pairs={{0,31},{1,0},{2,1},{3,2},{4,3},{5,4},{6,5},{7,6},{8,7},{9,8},{10,9... | collective-permute-start | bytes 98312 | tf_op jit(solution)/shard_map/ppermute | solution.py:559
  12.6 1.3 %collective-permute-done.10.left = f32[64,128]{1,0:T(8,128)S(1)} collective-permute-done((f32[64,128]{1,0:T(8,128)S(1)}, f32[64,128]{1,0:T(8,128)S(1)}, u32[]{:S(2)}, u32[]{:S(2)}) %collective-permute-start.10) | collective-permute-done | bytes 32800 | tf_op jit(solution)/shard_map/ppermute | solution.py:559
  13.9 0.0 collective-permute-done.11.right
  13.9 0.1 shard_map.87
  14.0 2.1 %collective-permute-start.15 = (f32[96,128]{1,0:T(8,128)S(1)}, f32[96,128]{1,0:T(8,128)S(1)}, u32[]{:S(2)}, u32[]{:S(2)}) collective-permute-start(f32[96,128]{1,0:T(8,128)S(1)} %get-tuple-element.527.own_strip), channel_id=1, source_target_pairs={{0,224},{32,0},{64,32},{96,64},{128,96},{160,128},{192,160},{224,1... | collective-permute-start | bytes 147464 | tf_op jit(solution)/shard_map/ppermute | solution.py:559
  16.2 0.0 collective-permute-start.12
  16.2 2.7 %collective-permute-start.13 = (f32[112,128]{1,0:T(8,128)S(1)}, f32[112,128]{1,0:T(8,128)S(1)}, u32[]{:S(2)}, u32[]{:S(2)}) collective-permute-start(f32[112,128]{1,0:T(8,128)S(1)} %get-tuple-element.526), channel_id=1, source_target_pairs={{0,192},{32,224},{64,0},{96,32},{128,64},{160,96},{192,128},{224,1... | collective-permute-start | bytes 172040 | tf_op jit(solution)/shard_map/ppermute | solution.py:559
  18.8 0.0 collective-permute-done.15.strip_a1
  18.8 1.0 %collective-permute-start.14 = (f32[96,128]{1,0:T(8,128)S(1)}, f32[96,128]{1,0:T(8,128)S(1)}, u32[]{:S(2)}, u32[]{:S(2)}) collective-permute-start(f32[96,128]{1,0:T(8,128)S(1)} %get-tuple-element.527.own_strip), channel_id=1, source_target_pairs={{0,32},{32,64},{64,96},{96,128},{128,160},{160,192},{192,224},{224... | collective-permute-start | bytes 147464 | tf_op jit(solution)/shard_map/ppermute | solution.py:559
  19.9 2.3 %collective-permute-done.14.strip_b1 = f32[96,128]{1,0:T(8,128)S(1)} collective-permute-done((f32[96,128]{1,0:T(8,128)S(1)}, f32[96,128]{1,0:T(8,128)S(1)}, u32[]{:S(2)}, u32[]{:S(2)}) %collective-permute-start.14) | collective-permute-done | bytes 49184 | tf_op jit(solution)/shard_map/ppermute | solution.py:559
  22.2 0.0 collective-permute-done.12.below2
  22.2 0.0 collective-permute-done.13.above2
  22.2 0.0 collective-permute-done.9.above1
  22.2 0.0 collective-permute-done.8.below1
  22.2 2.6 %shard_map.88 = (f32[6,64,512]{2,1,0:T(8,128)S(1)}, f32[1,128]{1,0:T(1,128)S(1)}) custom-call(f32[8,128]{1,0:T(8,128)S(1)} %get-tuple-element.520.shift_in, bf16[96,384]{1,0:T(8,128)(2,1)S(1)} %get-tuple-element.521.weight, f32[568,128]{1,0:T(8,128)S(1)} %get-tuple-element.522.near, f32[568,128]{1,0:T(8,128)S(1)} %collective-permute-done.8.below1, ...), custom_call_target="tpu_custom_call" | custom-call | tf_op jit(solution)/shard_map/pallas_call | solution.py:592
  24.8 0.1 broadcast_in_dim.114
  24.9 23.9 %all_to_all.53 = f32[256,1,128]{2,1,0:T(1,128)S(1)} all-to-all(f32[256,1,128]{2,1,0:T(1,128)S(1)} %broadcast_in_dim.114), channel_id=1, replica_groups=mesh['gx_0'=4,'gx_1'=2,'gy_0'=4,'gy_1'=8] {'gx_0','gx_1','gy_0','gy_1'}, dimensions={0} | all-to-all | bytes 262144 | tf_op jit(solution)/shard_map/all_to_all | solution.py:605
  48.8 1.3 %shard_map.89 = (f32[6,256,128]{2,1,0:T(8,128)}, f32[6,5]{1,0:T(8,128)}, f32[1,128]{1,0:T(1,128)S(1)}) custom-call(f32[8,128]{1,0:T(8,128)S(1)} %get-tuple-element.520.shift_in, f32[6,64,512]{2,1,0:T(8,128)S(1)} %get-tuple-element.528.powers, f32[256,128]{1,0:T(8,128)S(1)} %bitcast.494), custom_call_target="tpu_custom_call" | custom-call | tf_op jit(solution)/shard_map/pallas_call | solution.py:606
  50.1 0.2 while.41
Async XLA Ops:
  2.1 20.1 %collective-permute-start.9 = (f32[568,128]{1,0:T(8,128)S(1)}, f32[568,128]{1,0:T(8,128)S(1)}, u32[]{:S(2)}, u32[]{:S(2)}) collective-permute-start(f32[568,128]{1,0:T(8,128)S(1)} %get-tuple-element.522.near), channel_id=1, source_target_pairs={{0,224},{32,0},{64,32},{96,64},{128,96},{160,128},{192,160},{224,1... | collective-permute-start | bytes 872456 | tf_op jit(solution)/shard_map/ppermute | solution.py:559
  5.4 16.9 %collective-permute-start.8 = (f32[568,128]{1,0:T(8,128)S(1)}, f32[568,128]{1,0:T(8,128)S(1)}, u32[]{:S(2)}, u32[]{:S(2)}) collective-permute-start(f32[568,128]{1,0:T(8,128)S(1)} %get-tuple-element.522.near), channel_id=1, source_target_pairs={{0,32},{32,64},{64,96},{96,128},{128,160},{160,192},{192,224},{224... | collective-permute-start | bytes 872456 | tf_op jit(solution)/shard_map/ppermute | solution.py:559
  5.4 8.6 %collective-permute-start.10 = (f32[64,128]{1,0:T(8,128)S(1)}, f32[64,128]{1,0:T(8,128)S(1)}, u32[]{:S(2)}, u32[]{:S(2)}) collective-permute-start(f32[64,128]{1,0:T(8,128)S(1)} %get-tuple-element.523), channel_id=1, source_target_pairs={{0,1},{1,2},{2,3},{3,4},{4,5},{5,6},{6,7},{7,8},{8,9},{9,10},{10,1... | collective-permute-start | bytes 98312 | tf_op jit(solution)/shard_map/ppermute | solution.py:559
  6.5 7.4 %collective-permute-start.11 = (f32[64,128]{1,0:T(8,128)S(1)}, f32[64,128]{1,0:T(8,128)S(1)}, u32[]{:S(2)}, u32[]{:S(2)}) collective-permute-start(f32[64,128]{1,0:T(8,128)S(1)} %get-tuple-element.524), channel_id=1, source_target_pairs={{0,31},{1,0},{2,1},{3,2},{4,3},{5,4},{6,5},{7,6},{8,7},{9,8},{10,9... | collective-permute-start | bytes 98312 | tf_op jit(solution)/shard_map/ppermute | solution.py:559
  14.0 4.8 %collective-permute-start.15 = (f32[96,128]{1,0:T(8,128)S(1)}, f32[96,128]{1,0:T(8,128)S(1)}, u32[]{:S(2)}, u32[]{:S(2)}) collective-permute-start(f32[96,128]{1,0:T(8,128)S(1)} %get-tuple-element.527.own_strip), channel_id=1, source_target_pairs={{0,224},{32,0},{64,32},{96,64},{128,96},{160,128},{192,160},{224,1... | collective-permute-start | bytes 147464 | tf_op jit(solution)/shard_map/ppermute | solution.py:559
  16.2 6.1 %collective-permute-start.12 = (f32[112,128]{1,0:T(8,128)S(1)}, f32[112,128]{1,0:T(8,128)S(1)}, u32[]{:S(2)}, u32[]{:S(2)}) collective-permute-start(f32[112,128]{1,0:T(8,128)S(1)} %get-tuple-element.525), channel_id=1, source_target_pairs={{0,64},{32,96},{64,128},{96,160},{128,192},{160,224},{192,0},{224,... | collective-permute-start | bytes 172040 | tf_op jit(solution)/shard_map/ppermute | solution.py:559
  16.2 6.1 %collective-permute-start.13 = (f32[112,128]{1,0:T(8,128)S(1)}, f32[112,128]{1,0:T(8,128)S(1)}, u32[]{:S(2)}, u32[]{:S(2)}) collective-permute-start(f32[112,128]{1,0:T(8,128)S(1)} %get-tuple-element.526), channel_id=1, source_target_pairs={{0,192},{32,224},{64,0},{96,32},{128,64},{160,96},{192,128},{224,1... | collective-permute-start | bytes 172040 | tf_op jit(solution)/shard_map/ppermute | solution.py:559
  18.8 3.4 %collective-permute-start.14 = (f32[96,128]{1,0:T(8,128)S(1)}, f32[96,128]{1,0:T(8,128)S(1)}, u32[]{:S(2)}, u32[]{:S(2)}) collective-permute-start(f32[96,128]{1,0:T(8,128)S(1)} %get-tuple-element.527.own_strip), channel_id=1, source_target_pairs={{0,32},{32,64},{64,96},{96,128},{128,160},{160,192},{192,224},{224... | collective-permute-start | bytes 147464 | tf_op jit(solution)/shard_map/ppermute | solution.py:559
